TPU v7x, 32 devices: a whole 2x2x4 slice. The times are simulated.
32 devices in a mesh: dp: 8 (over z, y), tensor: 4 (over x, core).
Axes of the slice: x: 2, y: 2, z: 4, core: 2. Of those that a mesh axis runs over, the one named last changes fastest.
Arguments:
- hidden_in: bfloat16 [8, 1024, 1536], P('dp', 'tensor'), may hold values from -6 to 6
- d_out: bfloat16 [8, 1024, 1536], P('dp', 'tensor'), may hold values from -6 to 6
- in_gain: bfloat16 [1536], P('dp'), may hold values from 0.5 to 1.5
- w_zx: bfloat16 [1536, 2, 3072], P('dp', None, 'tensor'), may hold values from -0.15625 to 0.15625
- w_dt: bfloat16 [1536, 48], P('dp', 'tensor'), may hold values from -0.15625 to 0.15625
- w_bc: bfloat16 [1536, 256], P('dp'), may hold values from -0.15625 to 0.15625
- w_out: bfloat16 [1536, 3072], P('dp', 'tensor'), may hold values from -0.109375 to 0.109375
- conv_x_w: float32 [4, 3072], P(None, 'tensor'), may hold values from -0.5 to 0.5
- conv_x_b: float32 [3072], P('tensor'), may hold values from -0.5 to 0.5
- conv_bc_w: float32 [4, 256], replicated, may hold values from -0.5 to 0.5
- conv_bc_b: float32 [256], replicated, may hold values from -0.5 to 0.5
- dt_bias: float32 [48], P('tensor'), may hold values from -4.6 to -2.3
- a_log: float32 [48], P('tensor'), may hold values from 0 to 2.77
- d_skip: float32 [48], P('tensor'), may hold values from 0.5 to 1.5
- norm_scale: float32 [3072], P('tensor'), may hold values from 0.5 to 1.5
Outputs:
- block_out: bfloat16 [8, 1024, 1536], P('dp', 'tensor')
- d_hidden: float32 [8, 1024, 1536], P('dp', 'tensor')
- g_in_gain: float32 [1536], P('dp')
- g_w_zx: float32 [1536, 2, 3072], P('dp', None, 'tensor')
- g_w_dt: float32 [1536, 48], P('dp', 'tensor')
- input_output_weight_grad: float32 [1536, 256], P('dp')
- g_w_out: float32 [1536, 3072], P('dp', 'tensor')
- g_conv_x_w: float32 [4, 3072], P(None, 'tensor')
- g_conv_x_b: float32 [3072], P('tensor')
- g_conv_bc_w: float32 [4, 256], replicated
- g_conv_bc_b: float32 [256], replicated
- g_dt_bias: float32 [48], P('tensor')
- g_a_log: float32 [48], P('tensor')
- g_d_skip: float32 [48], P('tensor')
- g_norm_scale: float32 [3072], P('tensor')
All inputs are finite; a program needn't handle non-finite values.
Results may differ from a plain program's by a relative error of at most 0.0085.
Values may be sent and summed in bfloat16 or wider, within the bound.
A program may use at most 192 MiB of HBM per device.

v0:
```python
import jax
import jax.numpy as jnp
from jax import lax
from jax.sharding import PartitionSpec as P

SPAN = 256
INNER = 3072


EPSILON = 1e-05
HIGHEST = lax.Precision.HIGHEST


def causal_conv(inputs, kernel, conv_bias):
    kernel_taps = kernel.shape[0]
    seq_len = inputs.shape[1]
    padded = jnp.pad(inputs, ((0, 0), (kernel_taps - 1, 0), (0, 0)))
    result = conv_bias + kernel[0] * padded[:, 0:seq_len]
    for offset in range(1, kernel_taps):
        result = result + kernel[offset] * padded[:, offset : offset + seq_len]
    return result


def span_scan(values, timestep_widths, decay_rate, in_map, out_map):
    batch_seqs, seq_len, head_count, head_width = values.shape
    state_dim = in_map.shape[-1]
    blocks = seq_len // SPAN
    scaled_x = (values * timestep_widths[..., None]).reshape(
        batch_seqs, blocks, SPAN, head_count, head_width
    )
    decay_log = (timestep_widths * decay_rate).reshape(batch_seqs, blocks, SPAN, head_count)
    cumulative = jnp.cumsum(decay_log, axis=2)
    cumulative_h = jnp.moveaxis(cumulative, 3, 2)
    in_blocks = in_map.reshape(batch_seqs, blocks, SPAN, state_dim)
    out_blocks = out_map.reshape(batch_seqs, blocks, SPAN, state_dim)
    position = jnp.arange(SPAN)
    causal = position[:, None] >= position[None, :]
    log_gap = cumulative_h[..., :, None] - cumulative_h[..., None, :]
    within = jnp.where(causal, jnp.exp(jnp.where(causal, log_gap, 0.0)), 0.0)
    scores = jnp.einsum("scin,scjn->scij", out_blocks, in_blocks, precision=HIGHEST)
    mixed_weights = within * scores[:, :, None]
    diag_part = jnp.einsum("schij,scjhp->scihp", mixed_weights, scaled_x, precision=HIGHEST)
    last_step = cumulative_h[..., -1]
    to_end = jnp.exp(last_step[..., None] - cumulative_h)
    weighted = scaled_x * jnp.moveaxis(to_end, 2, 3)[..., None]
    block_states = jnp.einsum("scjhp,scjn->schpn", weighted, in_blocks, precision=HIGHEST)
    carried_state = jnp.zeros((batch_seqs, head_count, head_width, state_dim), jnp.float32)
    entering = []
    for block_index in range(blocks):
        entering.append(carried_state)
        carried_state = (
            jnp.exp(last_step[:, block_index])[..., None, None] * carried_state
            + block_states[:, block_index]
        )
    start_states = jnp.stack(entering, axis=1)
    carry_part = (
        jnp.einsum("scin,schpn->scihp", out_blocks, start_states, precision=HIGHEST)
        * jnp.exp(cumulative)[..., None]
    )
    return (diag_part + carry_part).reshape(batch_seqs, seq_len, head_count, head_width)


def mixer(
    gate_in,
    inner_in,
    delta_in,
    bc_proj,
    conv_x_w,
    conv_x_b,
    conv_bc_w,
    conv_bc_b,
    dt_bias,
    a_log,
    d_skip,
):
    x_conv = jax.nn.silu(causal_conv(inner_in, conv_x_w, conv_x_b))
    bc_conv = jax.nn.silu(causal_conv(bc_proj, conv_bc_w, conv_bc_b))
    state_dim = bc_conv.shape[-1] // 2
    timestep_widths = jax.nn.softplus(delta_in + dt_bias)
    decay_rate = -jnp.exp(a_log)
    batch_seqs, seq_len, channels = x_conv.shape
    head_count = timestep_widths.shape[-1]
    values = x_conv.reshape(batch_seqs, seq_len, head_count, channels // head_count)
    ssd_out = span_scan(
        values, timestep_widths, decay_rate, bc_conv[..., :state_dim], bc_conv[..., state_dim:]
    )
    ssd_out = ssd_out + d_skip[:, None] * values
    return ssd_out.reshape(batch_seqs, seq_len, channels) * jax.nn.silu(gate_in)


def in_rmsnorm(hidden, gain_vec):
    return (
        hidden * lax.rsqrt(jnp.mean(hidden * hidden, axis=-1, keepdims=True) + EPSILON) * gain_vec
    )


def local(
    hidden_in,
    d_out,
    in_gain,
    w_zx,
    w_dt,
    w_bc,
    w_out,
    conv_x_w,
    conv_x_b,
    conv_bc_w,
    conv_bc_b,
    dt_bias,
    a_log,
    d_skip,
    norm_scale,
):
    gathered = (
        lax.all_gather(in_gain, "dp", axis=0, tiled=True),
        lax.all_gather(w_zx, "dp", axis=0, tiled=True),
        lax.all_gather(w_dt, "dp", axis=0, tiled=True),
        lax.all_gather(w_bc, "dp", axis=0, tiled=True),
        lax.all_gather(w_out, "dp", axis=0, tiled=True),
    )
    gain_full, zx_full, dt_full, input_output_full, out_full = gathered
    hidden = hidden_in.astype(jnp.float32)
    normed_local, norm_pullback = jax.vjp(in_rmsnorm, hidden, gain_full.astype(jnp.float32))
    normalized_reduced = normed_local.astype(jnp.bfloat16)
    normed_seq = lax.all_gather(normalized_reduced, "tensor", axis=1, tiled=True)
    batch_seqs, seq_len, model_width = normed_seq.shape
    inner_local = zx_full.shape[2]
    normed_rows = normed_seq.reshape(-1, model_width)
    zx_matrix = zx_full.reshape(model_width, 2 * inner_local)
    both_proj = jnp.dot(normed_rows, zx_matrix, preferred_element_type=jnp.float32)
    gate_in = both_proj[:, :inner_local].reshape(batch_seqs, seq_len, inner_local)
    inner_in = both_proj[:, inner_local:].reshape(batch_seqs, seq_len, inner_local)
    delta_in = jnp.dot(normed_rows, dt_full, preferred_element_type=jnp.float32).reshape(
        batch_seqs, seq_len, -1
    )
    bc_proj = jnp.dot(normed_rows, input_output_full, preferred_element_type=jnp.float32).reshape(
        batch_seqs, seq_len, -1
    )
    gated_y, mix_pullback = jax.vjp(
        mixer,
        gate_in,
        inner_in,
        delta_in,
        bc_proj,
        conv_x_w,
        conv_x_b,
        conv_bc_w,
        conv_bc_b,
        dt_bias,
        a_log,
        d_skip,
    )
    square_sum = lax.psum(jnp.sum(gated_y * gated_y, axis=-1), "tensor")
    inverse = lax.rsqrt(square_sum / INNER + EPSILON)[..., None]
    normed_y = (gated_y * inverse * norm_scale).astype(jnp.bfloat16)
    y_rows = normed_y.reshape(-1, inner_local)
    partial_out = jnp.einsum("rk,dk->rd", y_rows, out_full, preferred_element_type=jnp.float32)
    branch = lax.psum_scatter(
        partial_out.reshape(batch_seqs, seq_len, model_width),
        "tensor",
        scatter_dimension=1,
        tiled=True,
    )
    block_out = (hidden + branch).astype(jnp.bfloat16)
    output_grad_sequence = lax.all_gather(d_out, "tensor", axis=1, tiled=True)
    dy_rows = output_grad_sequence.reshape(-1, model_width)
    g_w_out = jnp.einsum("rk,rd->dk", y_rows, dy_rows, preferred_element_type=jnp.float32)
    d_normed_y = jnp.dot(dy_rows, out_full, preferred_element_type=jnp.float32).reshape(
        batch_seqs, seq_len, inner_local
    )
    scaled = d_normed_y * norm_scale
    inner_sum = lax.psum(jnp.sum(scaled * gated_y, axis=-1), "tensor")[..., None]
    d_gated = inverse * scaled - gated_y * (inverse * inverse * inverse) * inner_sum / INNER
    g_norm_scale = jnp.sum((d_normed_y * gated_y * inverse).reshape(-1, inner_local), axis=0)
    (
        d_gate,
        d_inner,
        d_delta,
        d_bc,
        g_conv_x_w,
        g_conv_x_b,
        g_conv_bc_w,
        g_conv_bc_b,
        g_dt_bias,
        g_a_log,
        g_d_skip,
    ) = mix_pullback(d_gated)
    input_output_grad_total = lax.psum(d_bc, "tensor")
    d_proj = (
        jnp.concatenate([d_gate, d_inner], axis=-1)
        .astype(jnp.bfloat16)
        .reshape(-1, 2 * inner_local)
    )
    d_delta_low = d_delta.astype(jnp.bfloat16).reshape(-1, dt_full.shape[1])
    d_bc_low = input_output_grad_total.astype(jnp.bfloat16)
    partial_rows = jnp.einsum("rk,dk->rd", d_proj, zx_matrix, preferred_element_type=jnp.float32)
    partial_rows = partial_rows + jnp.einsum(
        "rh,dh->rd", d_delta_low, dt_full, preferred_element_type=jnp.float32
    )
    local_rows = lax.psum_scatter(
        partial_rows.reshape(batch_seqs, seq_len, model_width),
        "tensor",
        scatter_dimension=1,
        tiled=True,
    )
    rows_local = hidden_in.shape[1]
    row_start = lax.axis_index("tensor") * rows_local
    input_output_shard = lax.dynamic_slice_in_dim(d_bc_low, row_start, rows_local, 1)
    d_normed = local_rows + jnp.einsum(
        "nuo,ko->nuk", input_output_shard, input_output_full, preferred_element_type=jnp.float32
    )
    d_hidden_norm, g_gain_part = norm_pullback(d_normed)
    d_hidden = d_out.astype(jnp.float32) + d_hidden_norm
    g_w_zx = jnp.einsum(
        "rd,rk->dk", normed_rows, d_proj, preferred_element_type=jnp.float32
    ).reshape(model_width, 2, inner_local)
    g_w_dt = jnp.einsum("rd,rh->dh", normed_rows, d_delta_low, preferred_element_type=jnp.float32)
    input_output_weight_grad = jnp.einsum(
        "kao,kau->ou", normalized_reduced, input_output_shard, preferred_element_type=jnp.float32
    )
    reduced = (
        lax.psum_scatter(g_gain_part, "dp", scatter_dimension=0, tiled=True),
        lax.psum_scatter(g_w_zx, "dp", scatter_dimension=0, tiled=True),
        lax.psum_scatter(g_w_dt, "dp", scatter_dimension=0, tiled=True),
        lax.psum_scatter(input_output_weight_grad, "dp", scatter_dimension=0, tiled=True),
        lax.psum_scatter(g_w_out, "dp", scatter_dimension=0, tiled=True),
    )
    channel = lax.psum(
        (
            g_conv_x_w,
            g_conv_x_b,
            g_conv_bc_w,
            g_conv_bc_b,
            g_dt_bias,
            g_a_log,
            g_d_skip,
            g_norm_scale,
        ),
        "dp",
    )
    shared = lax.psum((reduced[0], reduced[3], channel[2], channel[3]), "tensor")
    return (
        block_out,
        d_hidden,
        shared[0],
        reduced[1],
        reduced[2],
        shared[1],
        reduced[4],
        channel[0],
        channel[1],
        shared[2],
        shared[3],
        channel[4],
        channel[5],
        channel[6],
        channel[7],
    )


def solution(mesh):
    in_specs = (
        P("dp", "tensor", None),
        P("dp", "tensor", None),
        P("dp"),
        P("dp", None, "tensor"),
        P("dp", "tensor"),
        P("dp", None),
        P("dp", "tensor"),
        P(None, "tensor"),
        P("tensor"),
        P(),
        P(),
        P("tensor"),
        P("tensor"),
        P("tensor"),
        P("tensor"),
    )
    out_specs = (
        P("dp", "tensor", None),
        P("dp", "tensor", None),
        P("dp"),
        P("dp", None, "tensor"),
        P("dp", "tensor"),
        P("dp", None),
        P("dp", "tensor"),
        P(None, "tensor"),
        P("tensor"),
        P(),
        P(),
        P("tensor"),
        P("tensor"),
        P("tensor"),
        P("tensor"),
    )
    return jax.shard_map(local, mesh=mesh, in_specs=in_specs, out_specs=out_specs, check_vma=False)
```

profile of v0, /device:TPU:0, one launch (start us, length us, event | category | flops | bytes accessed | tf_op | source)
XLA Modules:
  0.0 955.4 jit_solution(15111645828588249417)
XLA Ops:
  11.6 23.1 %all-reduce.27 = bf16[1536]{0:T(1024)(128)(2,1)S(1)} all-reduce(bf16[1536]{0:T(1024)(128)(2,1)S(1)} %dynamic-update-slice), channel_id=1, replica_groups=mesh['dp'=8,'tensor'=4] {'dp'}, use_global_device_ids=true, to_apply=%add.27 | all-reduce | flops 1536 | bytes 6144
  40.7 30.5 %all-gather = bf16[8,192,12]{1,2,0:T(8,128)(2,1)S(1)} all-gather(bf16[1,192,12]{1,2,0:T(8,128)(2,1)S(1)} %bitcast.381), channel_id=1, replica_groups=mesh['dp'=8,'tensor'=4] {'dp'}, dimensions={0}, use_global_device_ids=true | all-gather | bytes 41472 | tf_op jit(solution)/shard_map/all_gather | solution.py:117
  71.4 36.3 %all_gather.25 = bf16[1536,256]{1,0:T(8,128)(2,1)} all-gather(bf16[192,256]{1,0:T(8,128)(2,1)S(1)} %copy-done.51), channel_id=1, replica_groups=mesh['dp'=8,'tensor'=4] {'dp'}, dimensions={0}, use_global_device_ids=true | all-gather | bytes 884736 | tf_op jit(solution)/shard_map/all_gather | solution.py:118
  131.5 17.8 %all-gather.8.cloned.1.call-done = bf16[1536,2,768]{2,1,0:T(2,128)(2,1)} async-done(((bf16[192,2,768]{2,1,0:T(2,128)(2,1)}), bf16[1536,2,768]{2,1,0:T(2,128)(2,1)}) %all-gather.8.cloned.1.call-update) | async-done | bytes 4718608 | tf_op jit(solution)/shard_map/all_gather | solution.py:116
  189.5 14.4 %bitcast_add_fusion.1 = f32[1,4,256,12,64]{2,4,3,1,0:T(8,128)S(1)} fusion(f32[4,256,12,64]{1,3,2,0:T(8,128)S(1)} %fusion.96, f32[4,256,256]{2,1,0:T(8,128)S(1)} %copy-done.36, f32[4,12,256]{2,1,0:T(8,128)S(1)} %copy-done.52, pred[256,256]{1,0:T(8,128)(4,1)S(1)} %copy-done.54, f32[4,256,12,64]{1,0,3,2:T(4,128)S(1)} %copy-done.6, ...), kind=kOutput, calls=%fused_computation.37 | convolution fusion | flops 2430861312 | bytes 10698752 | tf_op jit(solution)/shard_map/jvp(schij,scjhp->scihp)/dot_general | solution.py:42
  217.3 7.0 psum.105
  230.3 8.5 multiply_reduce_fusion.1
  238.8 6.8 psum.106
  282.2 7.0 fusion.27
  290.8 21.9 %fusion.7 = (f32[4,12,256]{2,1,0:T(8,128)}, f32[4,12,256]{2,1,0:T(8,128)}, f32[4,256,256]{2,1,0:T(8,128)S(1)}) fusion(f32[4,256,256]{2,1,0:T(8,128)} %fusion.148, f32[4,12,256]{2,1,0:T(8,128)} %copy.273, pred[256,256]{1,0:T(8,128)(4,1)} %iota_compare_fusion, f32[4,256,12,64]{1,0,3,2:T(4,128)} %reshape.896, f32[4,256,12]{1,2,0:T(8,128)} %copy-done.33, ...), kind=kOutput, calls=%fused_computation.8 | convolution fusion | flops 2451021824 | bytes 8650752 | tf_op jit(solution)/shard_map/transpose(jvp(schij,scjhp->scihp))/dot_general | solution.py:42
  312.8 12.4 %bitcast_add_fusion = f32[1,4,256,12,64]{2,4,3,1,0:T(8,128)} fusion(f32[4,12,64,256]{3,2,1,0:T(8,128)S(1)} %copy-done.28, f32[4,256,256]{2,1,0:T(8,128)S(1)} %copy-done.37, f32[4,12,256]{2,1,0:T(8,128)S(1)} %copy-done.53, pred[256,256]{1,0:T(8,128)(4,1)S(1)} %copy-done.55, f32[4,12,64,256]{3,0,2,1:T(4,128)S(1)} %bitcast.345, f32[4,256,12]{1,2,0:T(8,128)S(1)} %copy-done.41), kind=kOutput, calls=%fused_computation.36 | convolution fusion | flops 2430074880 | bytes 10649600 | tf_op jit(solution)/shard_map/transpose(jvp(schij,scjhp->scihp))/dot_general | solution.py:42
  335.8 10.1 %reduce-window.16 = f32[1,4,12,2,128]{4,2,3,1,0:T(8,128)S(1)} reduce-window(f32[1,4,12,2,128]{4,2,3,1,0:T(8,128)S(1)} %copy.305, f32[]{:T(128)} %constant.24.clone.1), window={size=1x1x1x1x128 pad=0_0x0_0x0_0x0_0x0_127}, to_apply=%region_16.17 | reduce-window | flops 1560576 | bytes 98308 | tf_op jit(solution)/shard_map/reduce-window.2
  364.3 26.5 %all-reduce.35 = bf16[1,1024,256]{2,1,0:T(8,128)(2,1)} all-reduce(f32[1,1024,256]{2,1,0:T(8,128)} %pad_add_fusion.6), channel_id=1, replica_groups=mesh['dp'=8,'tensor'=4] {'tensor'}, use_global_device_ids=true, to_apply=%region_21.22 | all-reduce | flops 262144 | bytes 1572864 | tf_op jit(solution)/shard_map/psum | solution.py:188
  399.5 9.6 %multiply_reduce_fusion.4 = (f32[768]{0:T(1024)S(1)}, f32[768]{0:T(1024)S(1)}, f32[768]{0:T(1024)S(1)}, f32[768]{0:T(1024)S(1)}, f32[768]{0:T(1024)S(1)}, /*index=5*/f32[1,1024,768]{2,1,0:T(8,128)S(1)}) fusion(f32[1,1024,768]{2,1,0:T(8,128)} %copy-done.8, f32[1024,1536]{1,0:T(8,128)} %copy-done, f32[1,1024,768]{2,1,0:T(8,128)S(1)} %get-tuple-element.159, ...), kind=kLoop, calls=%fused_computation.64 | loop fusion | flops 16511232 | bytes 22038528 | tf_op jit(solution)/shard_map/transpose(jvp())/reduce_sum | solution.py:20
  428.6 7.5 fusion.53
  456.5 9.9 %fusion.24 = f32[1536,2,768]{2,0,1:T(8,128)} fusion(bf16[2,768,1024]{2,1,0:T(8,128)(2,1)} %bitcast.346, bf16[1,1024,1536]{2,1,0:T(8,128)(2,1)} %all-gather.6.cloned.1.call-done), kind=kOutput, calls=%fused_computation.34 | convolution fusion | flops 4831838208 | bytes 15728640 | tf_op jit(solution)/shard_map/rd,rk->dk/dot_general | solution.py:214
  481.0 44.8 %reduce-scatter.19.cloned.1.call-done = f32[192,12]{1,0:T(8,128)} async-done(((f32[1536,12]{1,0:T(8,128)}), f32[192,12]{1,0:T(8,128)}) %reduce-scatter.19.cloned.1.call-update) | async-done | bytes 9232
  527.4 58.7 %reduce-scatter.13.cloned.1.call-done = f32[1,256,1536]{2,1,0:T(8,128)} async-done(((f32[1,1024,1536]{2,1,0:T(8,128)}), f32[1,256,1536]{2,1,0:T(8,128)}) %reduce-scatter.13.cloned.1.call-update) | async-done | bytes 1572880 | tf_op jit(solution)/shard_map/reduce_scatter | solution.py:200
  588.5 38.1 %all-reduce.29 = (f32[1536]{0:T(1024)S(1)}, f32[4,768]{1,0:T(4,128)}, f32[768]{0:T(1024)}, f32[4,256]{1,0:T(4,128)S(1)}, f32[256]{0:T(256)S(1)}, /*index=5*/f32[...) all-reduce(f32[1536]{0:T(1024)S(1)} %get-tuple-element.117, ...), channel_id=4, replica_groups=mesh['dp'=8,'tensor'=4] {'dp'}, use_global_device_ids=true, to_apply=%region_24.25.clone | all-reduce | flops 7460 | bytes 59680
  626.7 7.4 all-reduce.30
  634.1 13.7 %reduce-scatter.11.cloned.1.call-done = f32[1,256,1536]{2,1,0:T(8,128)} async-done(((f32[1,1024,1536]{2,1,0:T(8,128)}), f32[1,256,1536]{2,1,0:T(8,128)}) %reduce-scatter.11.cloned.1.call-update) | async-done | bytes 1572880 | tf_op jit(solution)/shard_map/reduce_scatter | solution.py:158
  651.1 162.4 %reduce-scatter.15.cloned.1.call-done = f32[192,2,768]{2,0,1:T(8,128)} async-done(((f32[1536,2,768]{2,0,1:T(8,128)}), f32[192,2,768]{2,0,1:T(8,128)}) %reduce-scatter.15.cloned.1.call-update) | async-done | bytes 1179664 | tf_op jit(solution)/shard_map/reduce_scatter | solution.py:223
  816.7 30.1 %all-reduce.34.cloned.1.call-done = f32[192,256]{1,0:T(8,128)} async-done(((f32[192,256]{1,0:T(8,128)}), f32[192,256]{1,0:T(8,128)}) %all-reduce.34.cloned.1.call-update) | async-done | bytes 196624 | tf_op jit(solution)/shard_map/psum | solution.py:241
  846.8 99.9 %reduce-scatter.21.cloned.1.call-done = f32[192,768]{1,0:T(8,128)} async-done(((f32[1536,768]{1,0:T(8,128)}), f32[192,768]{1,0:T(8,128)}) %reduce-scatter.21.cloned.1.call-update) | async-done | bytes 589840
  (363 shorter events, 233.4 us)
Async XLA Ops:
  7.2 101.0 %copy-start.92 = (f32[12]{0:T(128)S(1)}, f32[12]{0:T(128)}, u32[]{:S(2)}) copy-start(f32[12]{0:T(128)} %param.26) | copy-start | bytes 148
  7.3 101.0 %all-gather.6.cloned.1.call-start = ((), (), s32[]{:S(2)}) async-start(), calls=%async_computation.6 | async-start | bytes 3932160 | tf_op jit(solution)/shard_map/all_gather | solution.py:125
  37.6 111.7 %all-gather.8.cloned.1.call-start = ((), (), s32[]{:S(2)}) async-start(), calls=%async_computation.7 | async-start | bytes 5308416 | tf_op jit(solution)/shard_map/all_gather | solution.py:116
  38.4 187.3 %all-gather.10.cloned.1.call-start = ((), (), s32[]{:S(2)}) async-start(), calls=%async_computation.8 | async-start | bytes 2654208 | tf_op jit(solution)/shard_map/all_gather | solution.py:119
  39.1 191.2 %all-gather.12.cloned.1.call-start = ((), (), s32[]{:S(2)}) async-start(), calls=%async_computation.10 | async-start | bytes 3932160 | tf_op jit(solution)/shard_map/all_gather | solution.py:165
  39.7 426.8 %reduce-scatter.17.cloned.1.call-start = ((), (), s32[]{:S(2)}) async-start(), calls=%async_computation.13 | async-start | bytes 1769472 | tf_op jit(solution)/shard_map/reduce_scatter | solution.py:225
  40.4 79.7 %copy-start.72 = (f32[1,256]{1,0:T(1,128)}, f32[1,256]{1,0:T(1,128)S(1)}, u32[]{:S(2)}) copy-start(f32[1,256]{1,0:T(1,128)S(1)} %get-tuple-element.178) | copy-start | bytes 3076
  40.4 79.7 %copy-start.74 = (f32[1,256]{1,0:T(1,128)}, f32[1,256]{1,0:T(1,128)S(1)}, u32[]{:S(2)}) copy-start(f32[1,256]{1,0:T(1,128)S(1)} %get-tuple-element.179) | copy-start | bytes 3076
  40.7 119.5 %copy-start.56 = (f32[768]{0:T(1024)}, f32[768]{0:T(1024)S(1)}, u32[]{:S(2)}) copy-start(f32[768]{0:T(1024)S(1)} %get-tuple-element.125) | copy-start | bytes 9220
  40.7 119.5 %copy-start.58 = (f32[768]{0:T(1024)}, f32[768]{0:T(1024)S(1)}, u32[]{:S(2)}) copy-start(f32[768]{0:T(1024)S(1)} %get-tuple-element.126) | copy-start | bytes 9220
  40.7 119.5 %copy-start.60 = (f32[768]{0:T(1024)}, f32[768]{0:T(1024)S(1)}, u32[]{:S(2)}) copy-start(f32[768]{0:T(1024)S(1)} %get-tuple-element.127) | copy-start | bytes 9220
  40.7 119.5 %copy-start.62 = (f32[768]{0:T(1024)}, f32[768]{0:T(1024)S(1)}, u32[]{:S(2)}) copy-start(f32[768]{0:T(1024)S(1)} %get-tuple-element.128) | copy-start | bytes 9220
  393.5 132.3 %reduce-scatter.19.cloned.1.call-start = ((), (), s32[]{:S(2)}) async-start(), calls=%async_computation.15 | async-start | bytes 884736
  422.7 163.4 %reduce-scatter.13.cloned.1.call-start = ((), (), s32[]{:S(2)}) async-start(), calls=%async_computation.11 | async-start | bytes 7864320 | tf_op jit(solution)/shard_map/reduce_scatter | solution.py:200
  439.8 208.0 %reduce-scatter.11.cloned.1.call-start = ((), (), s32[]{:S(2)}) async-start(), calls=%async_computation.9 | async-start | bytes 7864320 | tf_op jit(solution)/shard_map/reduce_scatter | solution.py:158
  448.0 365.5 %reduce-scatter.15.cloned.1.call-start = ((), (), s32[]{:S(2)}) async-start(), calls=%async_computation.12 | async-start | bytes 10616832 | tf_op jit(solution)/shard_map/reduce_scatter | solution.py:223
  466.4 380.4 %all-reduce.34.cloned.1.call-start = ((), (), s32[]{:S(2)}) async-start(), calls=%async_computation.14 | async-start | bytes 393216 | tf_op jit(solution)/shard_map/psum | solution.py:241
  467.0 479.7 %reduce-scatter.21.cloned.1.call-start = ((), (), s32[]{:S(2)}) async-start(), calls=%async_computation.16 | async-start | bytes 5308416
  479.8 106.3 %copy-start.17 = (bf16[1,256,1536]{2,1,0:T(8,128)(2,1)S(1)}, bf16[1,256,1536]{2,1,0:T(8,128)(2,1)}, u32[]{:S(2)}) copy-start(bf16[1,256,1536]{2,1,0:T(8,128)(2,1)} %param.15) | copy-start | bytes 2359300
  479.8 106.3 %copy-start.50 = (f32[1536]{0:T(1024)S(1)}, f32[1536]{0:T(1024)}, u32[]{:S(2)}) copy-start(f32[1536]{0:T(1024)} %copy-done.49) | copy-start | bytes 18436
  479.9 106.3 %copy-start.68 = (f32[256]{0:T(256)S(1)}, f32[256]{0:T(256)}, u32[]{:S(2)}) copy-start(f32[256]{0:T(256)} %copy-done.67) | copy-start | bytes 3076
  479.9 108.6 %copy-start.90 = (f32[768]{0:T(1024)S(1)}, f32[768]{0:T(1024)}, u32[]{:S(2)}) copy-start(f32[768]{0:T(1024)} %get-tuple-element.108) | copy-start | bytes 9220
  479.9 154.2 %copy-start.71 = (f32[256]{0:T(256)S(1)}, f32[256]{0:T(256)}, u32[]{:S(2)}) copy-start(f32[256]{0:T(256)} %copy-done.70) | copy-start | bytes 3076
  479.9 167.9 %copy-start.26 = (bf16[1,256,1536]{2,1,0:T(8,128)(2,1)S(1)}, bf16[1,256,1536]{2,1,0:T(8,128)(2,1)}, u32[]{:S(2)}) copy-start(bf16[1,256,1536]{2,1,0:T(8,128)(2,1)} %param.16) | copy-start | bytes 2359300
  (89 other events, 1260.4 us)
Sparse Core Ops, SparseCore 0:
  37.7 25.7 all-gather.5
  65.7 83.5 all-gather.7
  151.5 50.1 all-gather.9
  203.1 27.1 all-gather.11
  393.6 66.1 reduce-scatter.16
  463.6 62.1 reduce-scatter.18
  528.3 57.7 reduce-scatter.12
  588.6 59.1 reduce-scatter.10
  651.4 162.1 reduce-scatter.14
  815.7 31.0 all-reduce.33
  851.0 95.6 reduce-scatter.20
where the time goes:
time: 966 us; the launch traced here: 955 us
  waiting for transfers between devices  435 us (45%)
  blocking collectives  176 us (18%)
  matrix products  143 us (15%)
  local copies, waits for them, and re-layouts  95.6 us (10%)
  other arithmetic  88.6 us (9%)
  between operations  17.3 us (2%)
    reduce_scatter x1, waiting for transfers between devices, local(): lax.psum_scatter(g_w_zx, 'dp', scatter_dimension=0, tiled=True)  162 us
    unnamed x13, waiting for transfers between devices  147 us
    unnamed x2, blocking collectives  61.2 us
    reduce_scatter x1, waiting for transfers between devices, local(): lax.psum_scatter(partial_rows.reshape(batch_seqs, seq_len, model_width),...  58.7 us
    dot_general x3, matrix products, span_scan(): jnp.einsum('schij,scjhp->scihp', mixed_weights, scaled_x, precision=HIGHEST)  48.7 us
    all_gather x1, blocking collectives, local(): lax.all_gather(w_bc, 'dp', axis=0, tiled=True)  36.3 us
    unnamed x219, local copies, waits for them, and re-layouts  33.6 us
    all_gather x1, blocking collectives, local(): lax.all_gather(w_dt, 'dp', axis=0, tiled=True)  30.5 us
  transfers between devices with their start and end apart: 11, of which 8 were waited for; matrix products, arithmetic and copies ran while one was open for 19% of the time, Pallas kernels for 0%

commit v1 on v0

v1 whole, which is shorter than its diff:
```python
import jax
import jax.numpy as jnp
from jax import lax
from jax.experimental import pallas as pl
from jax.experimental.pallas import tpu as pltpu
from jax.sharding import PartitionSpec as P

Q = 128
STATE = 128
WIDTH = 64
NEG = -1e30
EPSILON = 1e-05
HIGHEST = lax.Precision.HIGHEST
F32 = jnp.float32
BF16 = jnp.bfloat16


def dot(a, b, dims=((1,), (0,)), precision=None):
    return lax.dot_general(a, b, (dims, ((), ())), precision=precision, preferred_element_type=F32)


def low(v):
    return v.astype(BF16)


def tri_masks():
    row = lax.broadcasted_iota(jnp.int32, (Q, Q), 0)
    col = lax.broadcasted_iota(jnp.int32, (Q, Q), 1)
    return row, col


def conv_block(buf, taps, bias):
    out = bias + taps[0:1] * buf[pl.ds(5, Q), :]
    for k in range(1, 4):
        out = out + taps[k : k + 1] * buf[pl.ds(5 + k, Q), :]
    return out


def softplus(v):
    return jnp.maximum(v, 0.0) + jnp.log1p(jnp.exp(-jnp.abs(v)))


def spread(columns, pair, low_half):
    first = jnp.broadcast_to(columns[:, 2 * pair : 2 * pair + 1], (columns.shape[0], 2 * WIDTH))
    second = jnp.broadcast_to(
        columns[:, 2 * pair + 1 : 2 * pair + 2], (columns.shape[0], 2 * WIDTH)
    )
    return first, second, jnp.where(low_half[: columns.shape[0]], first, second)


def forward_kernel(
    inner_ref, small_ref, xw_ref, xb_ref, bcw_ref, bcb_ref, bias_ref, alog_ref, skip_ref,
    y_ref, state_out_ref, xbuf, bcbuf, state, mixed, weighted,
):
    step = pl.program_id(0)
    heads = bias_ref.shape[1]

    @pl.when(step == 0)
    def _():
        state[...] = jnp.zeros_like(state)
        xbuf[0:8, :] = jnp.zeros((8, xbuf.shape[1]), F32)
        bcbuf[0:8, :] = jnp.zeros((8, bcbuf.shape[1]), F32)

    xbuf[8:, :] = inner_ref[...]
    bcbuf[8:, :] = small_ref[:, : 2 * STATE]
    row, col = tri_masks()
    causal = row >= col
    low_half = col < WIDTH
    pre_bc = conv_block(bcbuf, bcw_ref[...], bcb_ref[...])
    bc = low(pre_bc * jax.nn.sigmoid(pre_bc))
    b, c = bc[:, :STATE], bc[:, STATE:]
    dt = softplus(small_ref[:, 2 * STATE :] + bias_ref[...])
    decay = dt * -jnp.exp(alog_ref[...])
    cum = dot(causal.astype(F32), decay, precision=HIGHEST)
    cum_t = cum.T
    scores = dot(c, b, ((1,), (1,)))
    state_low = low(state[...])
    state_out_ref[0] = state[...]
    carried = dot(c, state_low)
    xw, xb = xw_ref[...], xb_ref[...]
    skip = skip_ref[...]
    for pair in range(heads // 2):
        sl = slice(2 * WIDTH * pair, 2 * WIDTH * (pair + 1))
        pre = xb[:, sl] + xw[0:1, sl] * xbuf[pl.ds(5, Q), sl]
        for k in range(1, 4):
            pre = pre + xw[k : k + 1, sl] * xbuf[pl.ds(5 + k, Q), sl]
        x = pre * jax.nn.sigmoid(pre)
        _, _, dt_e = spread(dt, pair, low_half)
        _, _, skip_e = spread(skip, pair, low_half)
        cum_0, cum_1, cum_e = spread(cum, pair, low_half)
        xh = x * dt_e
        parts = []
        for h, cum_h in ((2 * pair, cum_0), (2 * pair + 1, cum_1)):
            gap = cum_h - cum_t[h : h + 1, :]
            parts.append(low(jnp.exp(jnp.where(causal, gap, NEG)) * scores))
        xl = low(xh)
        zero = jnp.zeros_like(xl)
        stacked = jnp.concatenate([jnp.where(low_half, xl, zero), jnp.where(low_half, zero, xl)], 0)
        y = dot(jnp.concatenate(parts, 1), stacked)
        last = cum_e[Q - 1 : Q, :]
        y = y + carried[:, sl] * jnp.exp(cum_e) + skip_e * x
        y_ref[:, sl] = y
        weighted[:, sl] = low(xh * jnp.exp(last - cum_e))
        mixed[:, sl] = jnp.exp(last)
    state[...] = state[...] * mixed[...] + dot(b.T, weighted[...])
    xbuf[0:8, :] = xbuf[Q : Q + 8, :]
    bcbuf[0:8, :] = bcbuf[Q : Q + 8, :]


def full(shape):
    return pl.BlockSpec(shape, lambda i: (0,) * len(shape))


def mixer_forward(inner, small, xw, xb, bcw, bcb, bias, alog, skip):
    rows, channels = inner.shape
    blocks = rows // Q
    wide = small.shape[1]
    return pl.pallas_call(
        forward_kernel,
        name="mixer_forward",
        grid=(blocks,),
        in_specs=[
            pl.BlockSpec((Q, channels), lambda i: (i, 0)),
            pl.BlockSpec((Q, wide), lambda i: (i, 0)),
            full(xw.shape), full(xb.shape), full(bcw.shape), full(bcb.shape),
            full(bias.shape), full(alog.shape), full(skip.shape),
        ],
        out_specs=[
            pl.BlockSpec((Q, channels), lambda i: (i, 0)),
            pl.BlockSpec((1, STATE, channels), lambda i: (i, 0, 0)),
        ],
        out_shape=[
            jax.ShapeDtypeStruct((rows, channels), F32),
            jax.ShapeDtypeStruct((blocks, STATE, channels), F32),
        ],
        scratch_shapes=[
            pltpu.VMEM((Q + 8, channels), F32),
            pltpu.VMEM((Q + 8, 2 * STATE), F32),
            pltpu.VMEM((STATE, channels), F32),
            pltpu.VMEM((1, channels), F32),
            pltpu.VMEM((Q, channels), BF16),
        ],
        cost_estimate=pl.CostEstimate(
            flops=rows * channels * Q * 8, bytes_accessed=rows * channels * 16, transcendentals=rows * channels * 8
        ),
    )(inner, small, xw, xb, bcw, bcb, bias, alog, skip)


def backward_kernel(
    inner_ref, prev_ref, small_ref, sprev_ref, gy_ref, state_ref,
    xw_ref, xb_ref, bcw_ref, bcb_ref, bias_ref, alog_ref, skip_ref,
    dinner_ref, ddt_ref, dbc_ref, gxw_ref, gbcw_ref, ghead_ref,
    xbuf, bcbuf, dxbuf, dbcbuf, dstate, carried, back, rows_buf, sums, cgy, weighted, decay_row,
):
    step = pl.program_id(0)
    blocks = pl.num_programs(0)
    heads = bias_ref.shape[1]
    channels = inner_ref.shape[1]

    @pl.when(step == 0)
    def _():
        dstate[...] = jnp.zeros_like(dstate)
        dxbuf[Q:, :] = jnp.zeros((8, channels), F32)
        dbcbuf[Q:, :] = jnp.zeros((8, 2 * STATE), F32)
        gxw_ref[...] = jnp.zeros_like(gxw_ref)
        gbcw_ref[...] = jnp.zeros_like(gbcw_ref)
        ghead_ref[...] = jnp.zeros_like(ghead_ref)

    first = step == blocks - 1
    xbuf[0:8, :] = jnp.where(first, 0.0, prev_ref[...])
    bcbuf[0:8, :] = jnp.where(first, 0.0, sprev_ref[:, : 2 * STATE])
    xbuf[8:, :] = inner_ref[...]
    bcbuf[8:, :] = small_ref[:, : 2 * STATE]
    row, col = tri_masks()
    causal = row >= col
    causal_t = col >= row
    low_half = col < WIDTH
    pre_bc = conv_block(bcbuf, bcw_ref[...], bcb_ref[...])
    sig_bc = jax.nn.sigmoid(pre_bc)
    bc = low(pre_bc * sig_bc)
    b, c = bc[:, :STATE], bc[:, STATE:]
    raw = small_ref[:, 2 * STATE :] + bias_ref[...]
    dt = softplus(raw)
    a = -jnp.exp(alog_ref[...])
    cum = dot(causal.astype(F32), dt * a, precision=HIGHEST)
    cum_t = cum.T
    scores_t = dot(b, c, ((1,), (1,)))
    dstate_low = low(dstate[...])
    state_low = low(state_ref[0])
    carried[...] = dot(c, state_low)
    back[...] = dot(b, dstate_low)
    xw, xb = xw_ref[...], xb_ref[...]
    skip = skip_ref[...]
    dscores_t = jnp.zeros((Q, Q), F32)
    cols = jnp.zeros((Q, heads), F32)
    hot_row = lax.broadcasted_iota(jnp.int32, (2 * Q, heads), 0) // Q
    hot_col = lax.broadcasted_iota(jnp.int32, (2 * Q, heads), 1)
    for pair in range(heads // 2):
        sl = slice(2 * WIDTH * pair, 2 * WIDTH * (pair + 1))
        shifted = [xbuf[pl.ds(5 + k, Q), sl] for k in range(4)]
        pre = xb[:, sl] + xw[0:1, sl] * shifted[0]
        for k in range(1, 4):
            pre = pre + xw[k : k + 1, sl] * shifted[k]
        sig = jax.nn.sigmoid(pre)
        x = pre * sig
        _, _, dt_e = spread(dt, pair, low_half)
        _, _, skip_e = spread(skip, pair, low_half)
        cum_0, cum_1, cum_e = spread(cum, pair, low_half)
        last = cum_e[Q - 1 : Q, :]
        xh = x * dt_e
        xl = low(xh)
        gy = gy_ref[:, sl]
        gl = low(gy)
        zero = jnp.zeros_like(gl)
        g_stack = jnp.concatenate([jnp.where(low_half, gl, zero), jnp.where(low_half, zero, gl)], 0)
        dmixed_t = dot(xl, g_stack, ((1,), (1,)))
        mixes, zs = [], []
        for i, (h, cum_h) in enumerate(((2 * pair, cum_0), (2 * pair + 1, cum_1))):
            gap = cum_t[h : h + 1, :] - cum_h
            within = jnp.exp(jnp.where(causal_t, gap, NEG))
            mix = within * scores_t
            dm = dmixed_t[:, i * Q : (i + 1) * Q]
            dscores_t = dscores_t + dm * within
            z = low(dm * mix)
            zs.append(z)
            mixes.append(low(mix))
            rows_buf[h : h + 1, :] = jnp.sum(z.astype(F32), axis=0, keepdims=True)
        hot = (hot_col == hot_row + 2 * pair).astype(BF16)
        cols = cols + dot(jnp.concatenate(zs, 1), hot)
        dxh = dot(jnp.concatenate(mixes, 1), g_stack)
        to_end = jnp.exp(last - cum_e)
        from_state = to_end * back[:, sl]
        dxh = dxh + from_state
        grown = jnp.exp(cum_e) * gy
        cgy[:, sl] = low(grown)
        weighted[:, sl] = low(xh * to_end)
        sums[0:Q, sl] = low(grown * carried[:, sl])
        sums[Q : 2 * Q, sl] = low(xh * from_state)
        sums[2 * Q : 3 * Q, sl] = low(dxh * x)
        sums[3 * Q : 4 * Q, sl] = low(gy * x)
        decay_row[:, sl] = jnp.exp(last)
        dx = dxh * dt_e + skip_e * gy
        dpre = dx * (sig * (1.0 + pre * (1.0 - sig)))
        dxbuf[0:Q, sl] = dpre
        out = xw[3:4, sl] * dpre
        for k in range(3):
            out = out + xw[k : k + 1, sl] * dxbuf[pl.ds(3 - k, Q), sl]
        dinner_ref[:, sl] = low(out)
        for k in range(4):
            gxw_ref[k : k + 1, sl] += jnp.sum(dpre * shifted[k], axis=0, keepdims=True)
        gxw_ref[4:5, sl] += jnp.sum(dpre, axis=0, keepdims=True)
    head_of = lax.broadcasted_iota(jnp.int32, (channels, heads), 0) // WIDTH
    head = lax.broadcasted_iota(jnp.int32, (channels, heads), 1)
    head_hot = (head_of == head).astype(BF16)
    head_sums = dot(sums[...], head_hot)
    v, u = head_sums[0:Q], head_sums[Q : 2 * Q]
    t_x, t_skip = head_sums[2 * Q : 3 * Q], head_sums[3 * Q :]
    kept = jnp.sum(dstate[...] * state_ref[0], axis=0, keepdims=True) * decay_row[...]
    dlast = dot(jnp.broadcast_to(kept, (8, channels)), head_hot.astype(F32), precision=HIGHEST)[0:1]
    dlast = dlast + jnp.sum(u, axis=0, keepdims=True)
    dcum = rows_buf[0:heads, :].T - cols + v - u
    ddecay = dot(causal_t.astype(F32), dcum, precision=HIGHEST) + dlast
    ddt = (ddecay * a + t_x) * jax.nn.sigmoid(raw)
    ddt_ref[...] = low(ddt)
    ghead_ref[0:1, :] += jnp.sum(ddt, axis=0, keepdims=True)
    ghead_ref[1:2, :] += jnp.sum(ddecay * dt, axis=0, keepdims=True) * a
    ghead_ref[2:3, :] += jnp.sum(t_skip, axis=0, keepdims=True)
    dsl = low(dscores_t)
    dc = dot(dsl, b, ((0,), (0,))) + dot(cgy[...], state_low, ((1,), (1,)))
    db = dot(dsl, c) + dot(weighted[...], dstate_low, ((1,), (1,)))
    dstate[...] = dstate[...] * decay_row[...] + dot(c.T, cgy[...])
    dbc = jnp.concatenate([db, dc], 1)
    dpre = dbc * (sig_bc * (1.0 + pre_bc * (1.0 - sig_bc)))
    dbcbuf[0:Q, :] = dpre
    bcw = bcw_ref[...]
    out = bcw[3:4] * dpre
    for k in range(3):
        out = out + bcw[k : k + 1] * dbcbuf[pl.ds(3 - k, Q), :]
    dbc_ref[...] = out.astype(dbc_ref.dtype)
    for k in range(4):
        gbcw_ref[k : k + 1, :] += jnp.sum(dpre * bcbuf[pl.ds(5 + k, Q), :], axis=0, keepdims=True)
    gbcw_ref[4:5, :] += jnp.sum(dpre, axis=0, keepdims=True)
    dxbuf[Q:, :] = dxbuf[0:8, :]
    dbcbuf[Q:, :] = dbcbuf[0:8, :]


def mixer_backward(inner, small, gy, states, xw, xb, bcw, bcb, bias, alog, skip, dbc_dtype=F32):
    rows, channels = inner.shape
    blocks = rows // Q
    wide = small.shape[1]
    heads = bias.shape[1]
    at = lambda i: blocks - 1 - i
    before = lambda i: jnp.maximum(at(i) * (Q // 8) - 1, 0)
    return pl.pallas_call(
        backward_kernel,
        name="mixer_backward",
        grid=(blocks,),
        in_specs=[
            pl.BlockSpec((Q, channels), lambda i: (at(i), 0)),
            pl.BlockSpec((8, channels), lambda i: (before(i), 0)),
            pl.BlockSpec((Q, wide), lambda i: (at(i), 0)),
            pl.BlockSpec((8, wide), lambda i: (before(i), 0)),
            pl.BlockSpec((Q, channels), lambda i: (at(i), 0)),
            pl.BlockSpec((1, STATE, channels), lambda i: (at(i), 0, 0)),
            full(xw.shape), full(xb.shape), full(bcw.shape), full(bcb.shape),
            full(bias.shape), full(alog.shape), full(skip.shape),
        ],
        out_specs=[
            pl.BlockSpec((Q, channels), lambda i: (at(i), 0)),
            pl.BlockSpec((Q, heads), lambda i: (at(i), 0)),
            pl.BlockSpec((Q, 2 * STATE), lambda i: (at(i), 0)),
            full((5, channels)), full((5, 2 * STATE)), full((3, heads)),
        ],
        out_shape=[
            jax.ShapeDtypeStruct((rows, channels), BF16),
            jax.ShapeDtypeStruct((rows, heads), BF16),
            jax.ShapeDtypeStruct((rows, 2 * STATE), dbc_dtype),
            jax.ShapeDtypeStruct((5, channels), F32),
            jax.ShapeDtypeStruct((5, 2 * STATE), F32),
            jax.ShapeDtypeStruct((3, heads), F32),
        ],
        scratch_shapes=[
            pltpu.VMEM((Q + 8, channels), F32),
            pltpu.VMEM((Q + 8, 2 * STATE), F32),
            pltpu.VMEM((Q + 8, channels), F32),
            pltpu.VMEM((Q + 8, 2 * STATE), F32),
            pltpu.VMEM((STATE, channels), F32),
            pltpu.VMEM((Q, channels), F32),
            pltpu.VMEM((Q, channels), F32),
            pltpu.VMEM((16, Q), F32),
            pltpu.VMEM((4 * Q, channels), BF16),
            pltpu.VMEM((Q, channels), BF16),
            pltpu.VMEM((Q, channels), BF16),
            pltpu.VMEM((1, channels), F32),
        ],
        cost_estimate=pl.CostEstimate(
            flops=rows * channels * Q * 20, bytes_accessed=rows * channels * 20, transcendentals=rows * channels * 10
        ),
    )(inner, inner, small, small, gy, states, xw, xb, bcw, bcb, bias, alog, skip)


def local(
    hidden_in, d_out, in_gain, w_zx, w_dt, w_bc, w_out,
    conv_x_w, conv_x_b, conv_bc_w, conv_bc_b, dt_bias, a_log, d_skip, norm_scale,
):
    _, rows_local, width = hidden_in.shape
    inner_local = w_zx.shape[2]
    heads = w_dt.shape[1]
    tensor_index = lax.axis_index("tensor")
    parts = lax.axis_size("tensor")
    hidden_bf = lax.all_gather(hidden_in[0], "tensor", axis=0, tiled=True)
    first_pack = jnp.concatenate([w_zx[:, 1, :], w_bc, w_dt, in_gain[:, None]], 1)
    first = lax.all_gather(first_pack, "dp", axis=0, tiled=True)
    second_pack = jnp.concatenate([w_zx[:, 0, :], w_out], 1)
    second = lax.all_gather(second_pack, "dp", axis=0, tiled=True)
    dout_all = lax.all_gather(d_out[0], "tensor", axis=0, tiled=True)
    w_inner = first[:, :inner_local]
    w_small = first[:, inner_local : inner_local + 2 * STATE + heads]
    gain = first[:, -1].astype(F32)[None]
    w_gate, w_o = second[:, :inner_local], second[:, inner_local:]

    hidden = hidden_bf.astype(F32)
    rh = lax.rsqrt(jnp.mean(hidden * hidden, axis=-1, keepdims=True) + EPSILON)
    xn = low(hidden * rh * gain)
    inner = dot(xn, w_inner)
    small = dot(xn, w_small)
    params = (
        conv_x_w, conv_x_b[None], conv_bc_w, conv_bc_b[None], dt_bias[None], a_log[None], d_skip[None],
    )
    y, states = mixer_forward(inner, small, *params)
    gate = dot(xn, w_gate)
    dyn = dot(dout_all, w_o)
    sig = jax.nn.sigmoid(gate)
    act = gate * sig
    gated = y * act
    scale = norm_scale[None]
    scaled = dyn * scale
    sums = lax.psum(jnp.stack([jnp.sum(gated * gated, -1), jnp.sum(scaled * gated, -1)]), "tensor")
    channels = inner_local * parts
    r = lax.rsqrt(sums[0] / channels + EPSILON)[:, None]
    yn = low(gated * r * scale)
    d_gated = r * scaled - gated * (r * r * r) * sums[1][:, None] / channels
    g_scale = jnp.sum(dyn * gated * r, axis=0)
    gy = d_gated * act
    d_gate = low(d_gated * y * (sig * (1.0 + gate * (1.0 - sig))))
    g_out = low(dot(dout_all, yn, ((0,), (0,))))
    g_gate = low(dot(xn, d_gate, ((0,), (0,))))
    early = lax.psum_scatter(
        jnp.concatenate([g_gate, g_out], 1), "dp", scatter_dimension=0, tiled=True
    ).astype(F32)
    partial_out = low(dot(yn, w_o, ((1,), (1,))))
    branch = lax.psum_scatter(partial_out, "tensor", scatter_dimension=0, tiled=True)
    hidden_own = hidden_in[0].astype(F32)
    block_out = low(hidden_own + branch.astype(F32))

    d_inner, d_dt, d_bc, g_x, g_bc, g_head = mixer_backward(
        inner, small, gy, states, *params, dbc_dtype=BF16
    )
    d_bc_low = lax.psum(d_bc, "tensor")
    own_columns = 2 * STATE // parts
    d_bc_own = lax.dynamic_slice_in_dim(d_bc_low, tensor_index * own_columns, own_columns, 1)
    late = jnp.concatenate([d_inner, d_bc_own, d_dt], 1)
    g_late = low(dot(xn, late, ((0,), (0,))))
    late_sum = lax.psum_scatter(g_late, "dp", scatter_dimension=0, tiled=True).astype(F32)
    w_small_own = jnp.concatenate(
        [
            lax.dynamic_slice_in_dim(first, inner_local + tensor_index * own_columns, own_columns, 1),
            w_small[:, 2 * STATE :],
        ],
        1,
    )
    d_xn = dot(d_gate, w_gate, ((1,), (1,))) + dot(d_inner, w_inner, ((1,), (1,)))
    d_xn = d_xn + dot(late[:, inner_local:], w_small_own, ((1,), (1,)))
    d_normed = lax.psum_scatter(low(d_xn), "tensor", scatter_dimension=0, tiled=True).astype(F32)
    rh_own = lax.rsqrt(jnp.mean(hidden_own * hidden_own, axis=-1, keepdims=True) + EPSILON)
    weighted = d_normed * gain
    g_gain = jnp.sum(d_normed * hidden_own * rh_own, axis=0)
    inner_sum = jnp.sum(weighted * hidden_own, axis=-1, keepdims=True)
    d_hidden = (
        d_out[0].astype(F32) + rh_own * weighted - hidden_own * (rh_own * rh_own * rh_own) * inner_sum / width
    )
    flat = jnp.concatenate(
        [g_gain, g_bc.reshape(-1), g_x.reshape(-1), g_scale, g_head.reshape(-1)]
    )
    flat = lax.psum(flat, "dp")
    shared_size = width + 5 * 2 * STATE
    shared = lax.psum(flat[:shared_size], "tensor")
    own = lax.dynamic_slice_in_dim(shared, lax.axis_index("dp") * in_gain.shape[0], in_gain.shape[0], 0)
    g_bc = shared[width:].reshape(5, 2 * STATE)
    g_x = flat[shared_size : shared_size + 5 * inner_local].reshape(5, inner_local)
    rest = flat[shared_size + 5 * inner_local :]
    g_scale = rest[:inner_local]
    g_head = rest[inner_local:].reshape(3, heads)
    g_w_bc = lax.all_gather(late_sum[:, inner_local : inner_local + own_columns], "tensor", axis=1, tiled=True)
    g_zx = jnp.stack([early[:, :inner_local], late_sum[:, :inner_local]], 1)
    return (
        block_out[None],
        d_hidden[None],
        own,
        g_zx,
        late_sum[:, inner_local + own_columns :],
        g_w_bc,
        early[:, inner_local:],
        g_x[:4],
        g_x[4],
        g_bc[:4],
        g_bc[4],
        g_head[0],
        g_head[1],
        g_head[2],
        g_scale,
    )


def solution(mesh):
    tokens = P("dp", "tensor", None)
    specs = (
        tokens,
        tokens,
        P("dp"),
        P("dp", None, "tensor"),
        P("dp", "tensor"),
        P("dp", None),
        P("dp", "tensor"),
        P(None, "tensor"),
        P("tensor"),
        P(),
        P(),
        P("tensor"),
        P("tensor"),
        P("tensor"),
        P("tensor"),
    )
    return jax.shard_map(local, mesh=mesh, in_specs=specs, out_specs=specs, check_vma=False)
```

time: 966 us -> 574 us (0.59); the launches traced: 955 us -> 573 us
  blocking collectives: 176 us -> 59.2 us
  matrix products: 143 us -> 56.6 us
  waiting for transfers between devices: 435 us -> 357 us
  local copies, waits for them, and re-layouts: 95.6 us -> 24.7 us
  other arithmetic: 88.6 us -> 20.3 us
  Pallas kernels: 0 us -> 40.8 us
    reduce_scatter x4 -> x2, waiting for transfers between devices: 235 us -> 31.1 us  [the longest x1 31 us: local(): lax.psum_scatter(low(d_xn), 'tensor', scatter_dimension=0, tiled=True)]
    all_gather x4, waiting for transfers between devices: 22.4 us -> 171 us  [the longest x1 64.7 us: local(): first = lax.all_gather(first_pack, 'dp', axis=0, tiled=True)]
    dot_general x23 -> x11, matrix products: 141 us -> 56.6 us  [dot(): lax.dot_general(a, b, (dims, ((), ())), precision=precision, preferred_el...]
    unnamed x2 -> x0, blocking collectives: 61.2 us -> none
    all_gather x2 -> x1, blocking collectives: 66.8 us -> 5.77 us  [local(): lax.all_gather(late_sum[:, inner_local:inner_local + own_columns], 'tenso...]
    pallas_call x0 -> x2, Pallas kernels: none -> 40.8 us  [the longest x1 27.4 us: mixer_backward(): pl.pallas_call(backward_kernel, name='mixer_backward', grid=(blocks,), in...]
    reduce_sum x11 -> x3, other arithmetic: 37 us -> 4.55 us  [the longest x1 2.72 us: local(): rh = lax.rsqrt(jnp.mean(hidden * hidden, axis=-1, keepdims=True) + EPSILON)]
    reshape x11 -> x3, local copies, waits for them, and re-layouts: 31.2 us -> 0.09 us  [the longest x1 0.08 us: local(): g_head.reshape(-1)]
  transfers between devices with their start and end apart: 11 -> 9, of which waited for: 8 -> 8; matrix products, arithmetic and copies ran while one was open for 19% -> 12% of each run, Pallas kernels for 0% -> 2%
where the time goes in v1:
time: 574 us; the launch traced here: 573 us
  waiting for transfers between devices  357 us (62%)
  blocking collectives  59.2 us (10%)
  matrix products  56.6 us (10%)
  Pallas kernels  40.8 us (7%)
  local copies, waits for them, and re-layouts  24.7 us (4%)
  other arithmetic  20.3 us (4%)
  between operations  14.3 us (2%)
    unnamed x11, waiting for transfers between devices  119 us
    all_gather x1, waiting for transfers between devices, local(): first = lax.all_gather(first_pack, 'dp', axis=0, tiled=True)  64.7 us
    all_gather x1, waiting for transfers between devices, local(): second = lax.all_gather(second_pack, 'dp', axis=0, tiled=True)  57.4 us
    dot_general x11, matrix products, dot(): lax.dot_general(a, b, (dims, ((), ())), precision=precision, preferred_el...  56.6 us
    psum x1, blocking collectives, local(): flat = lax.psum(flat, 'dp')  37.1 us
    psum x1, waiting for transfers between devices, local(): d_bc_low = lax.psum(d_bc, 'tensor')  34.6 us
    reduce_scatter x1, waiting for transfers between devices, local(): lax.psum_scatter(low(d_xn), 'tensor', scatter_dimension=0, tiled=True)  31 us
    pallas_call x1, Pallas kernels, mixer_backward(): pl.pallas_call(backward_kernel, name='mixer_backward', grid=(blocks,), in...  27.4 us
  transfers between devices with their start and end apart: 9, of which 8 were waited for; matrix products, arithmetic and copies ran while one was open for 12% of the time, Pallas kernels for 2%

profile of v1, /device:TPU:0, one launch (start us, length us, event | category | flops | bytes accessed | tf_op | source)
XLA Modules:
  0.0 573.1 jit_solution(14126746026441355915)
XLA Ops:
  13.7 27.2 %all-gather.11.cloned.1.call-done = bf16[1,1024,1536]{2,1,0:T(8,128)(2,1)} async-done(((bf16[1,256,1536]{2,1,0:T(8,128)(2,1)}), bf16[1,1024,1536]{2,1,0:T(8,128)(2,1)}) %all-gather.11.cloned.1.call-update) | async-done | bytes 3145744 | tf_op jit(solution)/shard_map/all_gather | solution.py:351
  43.6 64.7 %all-gather.7.cloned.1.call-done = bf16[1536,1037]{1,0:T(8,128)(2,1)} async-done(((bf16[192,1037]{1,0:T(8,128)(2,1)}), bf16[1536,1037]{1,0:T(8,128)(2,1)}) %all-gather.7.cloned.1.call-update) | async-done | bytes 3185680 | tf_op jit(solution)/shard_map/all_gather | solution.py:353
  109.6 4.4 fusion.39.small_ref.sprev_ref
  114.0 4.3 fusion.20.inner_ref.prev_ref
  118.3 13.4 %mixer_forward.1 = (f32[1024,768]{1,0:T(8,128)}, f32[8,128,768]{2,1,0:T(8,128)}) custom-call(f32[1024,768]{1,0:T(8,128)} %fusion.20.inner_ref.prev_ref, f32[1024,268]{1,0:T(8,128)} %fusion.39.small_ref.sprev_ref, f32[4,768]{1,0:T(4,128)} %xw_ref.3, f32[1,768]{1,0:T(1,128)} %broadcast_in_dim.31.xb_ref, f32[4,256]{1,0:T(4,128)} %bcw_ref.3, f32[1,256]{1,0:T(1,128)} %bitcast.81, ...), custom_call_target="tpu_custom_call" | custom-call | flops 805306368 | bytes 12582912 | tf_op jit(solution)/shard_map/mixer_forward/pallas_call | solution.py:118
  131.7 57.4 %all-gather.9.cloned.1.call-done = bf16[1536,1536]{1,0:T(8,128)(2,1)} async-done(((bf16[192,1536]{1,0:T(8,128)(2,1)}), bf16[1536,1536]{1,0:T(8,128)(2,1)}) %all-gather.9.cloned.1.call-update) | async-done | bytes 4718608 | tf_op jit(solution)/shard_map/all_gather | solution.py:355
  189.1 6.1 %fusion.16 = f32[1024,768]{1,0:T(8,128)} fusion(bf16[1536,1536]{1,0:T(8,128)(2,1)} %all-gather.9.cloned.1.call-done, bf16[1,1024,1536]{2,1,0:T(8,128)(2,1)S(1)} %copy-done.1, f32[1536]{0:T(1024)S(1)} %convert_reduce_fusion, f32[1024]{0:T(1024)S(1)} %add_rsqrt_fusion), kind=kOutput, calls=%fused_computation.35 | convolution fusion | flops 2422210560 | bytes 8660992 | tf_op jit(solution)/shard_map/dot_general | solution.py:19
  195.2 22.2 %all-gather.13.cloned.1.call-done = bf16[1,1024,1536]{2,1,0:T(8,128)(2,1)} async-done(((bf16[1,256,1536]{2,1,0:T(8,128)(2,1)}), bf16[1,1024,1536]{2,1,0:T(8,128)(2,1)}) %all-gather.13.cloned.1.call-update) | async-done | bytes 3145744 | tf_op jit(solution)/shard_map/all_gather | solution.py:356
  217.4 9.9 %multiply_reduce_fusion.1 = (f32[1024]{0:T(1024)S(1)}, f32[1024]{0:T(1024)S(1)}, f32[1024,768]{1,0:T(8,128)}, f32[768,1024]{0,1:T(8,128)}) fusion(f32[768]{0:T(1024)S(1)} %copy-done.13, f32[1024,768]{1,0:T(8,128)} %get-tuple-element.23, f32[1024,768]{1,0:T(8,128)} %fusion.16, bf16[1536,1536]{1,0:T(8,128)(2,1)} %all-gather.9.cloned.1.call-done, ...), kind=kOutput, calls=%fused_computation.27 | convolution fusion | flops 2423781376 | bytes 18099200 | tf_op jit(solution)/shard_map/dot_general | solution.py:19
  227.3 6.2 %psum.28 = f32[2,1024]{1,0:T(2,128)S(1)} all-reduce(f32[2,1024]{1,0:T(2,128)S(1)} %pad_maximum_fusion.3), channel_id=1, replica_groups=mesh['dp'=8,'tensor'=4] {'tensor'}, use_global_device_ids=true, to_apply=%region_3.0 | all-reduce | flops 2048 | bytes 16384 | tf_op jit(solution)/shard_map/psum | solution.py:378
  233.5 7.3 %fusion.38 = (f32[1024,768]{1,0:T(8,128)}, bf16[1024,768]{1,0:T(8,128)(2,1)}, f32[768]{0:T(1024)S(1)}) fusion(f32[1024]{0:T(1024)S(1)} %bitcast.78, f32[1024,768]{1,0:T(8,128)} %get-tuple-element.80, f32[768,1024]{0,1:T(8,128)} %get-tuple-element.97, f32[1024]{0:T(1024)S(1)} %multiply_multiply_fusion, f32[1024]{0:T(1024)S(1)} %bitcast.75, ...), kind=kLoop, calls=%fused_computation.59 | loop fusion | flops 16514304 | bytes 17319936 | tf_op jit(solution)/shard_map/mul | solution.py:384
  240.8 27.4 %mixer_backward.1 = (bf16[1024,768]{1,0:T(8,128)(2,1)}, bf16[1024,12]{1,0:T(8,128)(2,1)}, bf16[1024,256]{1,0:T(8,128)(2,1)}, f32[5,768]{1,0:T(8,128)}, f32[5,256]{1,0:T(8,128)}, /*index=5*/f32[3,12]{1,0:T(4,128)}) custom-call(f32[1024,768]{1,0:T(8,128)} %fusion.20.inner_ref.prev_ref, f32[1024,768]{1,0:T(8,128)} %fusion.20.inner_ref.prev_ref, ...), custom_call_target="tpu_custom_call" | custom-call | flops 2013265920 | bytes 15728640 | tf_op jit(solution)/shard_map/mixer_backward/pallas_call | solution.py:294
  268.3 34.6 %all-reduce.2.cloned.1.call-done = bf16[1024,256]{1,0:T(8,128)(2,1)} async-done(((bf16[1024,256]{1,0:T(8,128)(2,1)}), bf16[1024,256]{1,0:T(8,128)(2,1)}) %all-reduce.2.cloned.1.call-update) | async-done | bytes 524304 | tf_op jit(solution)/shard_map/psum | solution.py:399
  304.0 6.7 %convolution_convert_fusion.1 = bf16[1536,844]{1,0:T(8,128)(2,1)} fusion(bf16[1024,12]{1,0:T(8,128)(2,1)} %get-tuple-element.27, bf16[1024,64]{1,0:T(8,128)(2,1)S(1)} %constant_dynamic-slice_fusion.1, bf16[1024,768]{1,0:T(8,128)(2,1)} %get-tuple-element.25, bf16[1,1024,1536]{2,1,0:T(8,128)(2,1)S(1)} %copy-done.1, f32[1536]{0:T(1024)S(1)} %convert_reduce_fusion, ...), kind=kOutput, calls=%fused_computation.8 | convolution fusion | flops 2667767808 | bytes 7477248 | tf_op jit(solution)/shard_map/dot_general | solution.py:19
  312.2 4.9 fusion.18
  323.0 6.9 %convolution_convert_fusion = bf16[1024,1536]{1,0:T(8,128)(2,1)} fusion(bf16[1536,1536]{1,0:T(8,128)(2,1)} %all-gather.9.cloned.1.call-done, f32[1024,768]{1,0:T(8,128)} %get-tuple-element.80, f32[1024]{0:T(1024)S(1)} %bitcast.76, f32[768]{0:T(1024)S(1)} %copy-done.13), kind=kOutput, calls=%fused_computation.7 | convolution fusion | flops 2419851264 | bytes 8657920 | tf_op jit(solution)/shard_map/dot_general | solution.py:19
  330.0 4.9 convolution_convert_fusion.3
  340.5 6.6 %copy.76 = bf16[1536,1536]{1,0:T(8,128)(2,1)} copy(bf16[1536,1536]{0,1:T(8,128)(2,1)} %pad_maximum_fusion) | data formatting | bytes 9437184
  348.6 34.2 %reduce-scatter.15.cloned.1.call-done = bf16[192,844]{1,0:T(8,128)(2,1)} async-done(((bf16[1536,844]{1,0:T(8,128)(2,1)}), bf16[192,844]{1,0:T(8,128)(2,1)}) %reduce-scatter.15.cloned.1.call-update) | async-done | bytes 324112
  384.7 5.8 %all_gather.19 = f32[192,256]{0,1:T(8,128)S(1)} all-gather(f32[192,64]{0,1:T(8,128)S(1)} %slice.149), channel_id=1, replica_groups=mesh['dp'=8,'tensor'=4] {'tensor'}, dimensions={1}, use_global_device_ids=true | all-gather | bytes 245760 | tf_op jit(solution)/shard_map/all_gather | solution.py:434
  391.3 31.0 %reduce-scatter.11.cloned.1.call-done = bf16[256,1536]{1,0:T(8,128)(2,1)} async-done(((bf16[1024,1536]{1,0:T(8,128)(2,1)}), bf16[256,1536]{1,0:T(8,128)(2,1)}) %reduce-scatter.11.cloned.1.call-update) | async-done | bytes 786448 | tf_op jit(solution)/shard_map/reduce_scatter | solution.py:414
  424.0 37.1 %psum.30 = f32[7460]{0:T(1024)S(1)} all-reduce(f32[7460]{0:T(1024)S(1)} %constant_dynamic-update-slice_fusion), channel_id=1, replica_groups=mesh['dp'=8,'tensor'=4] {'dp'}, use_global_device_ids=true, to_apply=%region_11.0 | all-reduce | flops 7460 | bytes 59680 | tf_op jit(solution)/shard_map/psum | solution.py:425
  461.1 10.2 %psum.31 = f32[2816]{0:T(1024)S(1)} all-reduce(f32[2816]{0:T(1024)S(1)} %slice.145), channel_id=1, replica_groups=mesh['dp'=8,'tensor'=4] {'tensor'}, use_global_device_ids=true, to_apply=%region_12.0 | all-reduce | flops 2816 | bytes 22528 | tf_op jit(solution)/shard_map/psum | solution.py:427
  478.4 83.9 %reduce-scatter.13.cloned.1.call-done = bf16[192,1536]{1,0:T(8,128)(2,1)} async-done(((bf16[1536,1536]{1,0:T(8,128)(2,1)}), bf16[192,1536]{1,0:T(8,128)(2,1)}) %reduce-scatter.13.cloned.1.call-update) | async-done | bytes 589840
  (115 shorter events, 41.4 us)
Async XLA Ops:
  7.2 3.1 copy-start.15
  7.2 3.2 copy-start.10
  7.2 3.4 copy-start.8
  7.2 4.3 copy-start.6
  7.2 33.6 %all-gather.11.cloned.1.call-start = ((), (), s32[]{:S(2)}) async-start(), calls=%async_computation.9 | async-start | bytes 3932160 | tf_op jit(solution)/shard_map/all_gather | solution.py:351
  8.0 100.3 %all-gather.7.cloned.1.call-start = ((), (), s32[]{:S(2)}) async-start(), calls=%async_computation.4 | async-start | bytes 3981312 | tf_op jit(solution)/shard_map/all_gather | solution.py:353
  10.3 2.8 copy-start.12
  11.5 177.6 %all-gather.9.cloned.1.call-start = ((), (), s32[]{:S(2)}) async-start(), calls=%async_computation.5 | async-start | bytes 5308416 | tf_op jit(solution)/shard_map/all_gather | solution.py:355
  12.4 205.0 %all-gather.13.cloned.1.call-start = ((), (), s32[]{:S(2)}) async-start(), calls=%async_computation.10 | async-start | bytes 3932160 | tf_op jit(solution)/shard_map/all_gather | solution.py:356
  13.0 289.9 %all-reduce.2.cloned.1.call-start = ((), (), s32[]{:S(2)}) async-start(), calls=%async_computation.7 | async-start | bytes 1048576 | tf_op jit(solution)/shard_map/psum | solution.py:399
  40.9 68.7 %copy-start.1 = (bf16[1,1024,1536]{2,1,0:T(8,128)(2,1)S(1)}, bf16[1,1024,1536]{2,1,0:T(8,128)(2,1)}, u32[]{:S(2)}) copy-start(bf16[1,1024,1536]{2,1,0:T(8,128)(2,1)} %all-gather.11.cloned.1.call-done) | copy-start | bytes 9437188
  109.6 4.4 copy-start.4
  131.7 85.7 %copy-start.13 = (f32[768]{0:T(1024)S(1)}, f32[768]{0:T(1024)}, u32[]{:S(2)}) copy-start(f32[768]{0:T(1024)} %param.29) | copy-start | bytes 9220
  268.2 114.6 %reduce-scatter.15.cloned.1.call-start = ((), (), s32[]{:S(2)}) async-start(), calls=%async_computation.12 | async-start | bytes 3096576
  310.7 111.7 %reduce-scatter.11.cloned.1.call-start = ((), (), s32[]{:S(2)}) async-start(), calls=%async_computation.8 | async-start | bytes 3932160 | tf_op jit(solution)/shard_map/reduce_scatter | solution.py:414
  310.7 6.4 %slice-start.1 = ((s8[4718592]{0:T(1024)(128)(4,1)}), s8[4194304]{0:T(1024)(128)(4,1)S(1)}, s32[]{:S(2)}) async-start(s8[4718592]{0:T(1024)(128)(4,1)} %bitcast.89), calls=%async_computation.14 | async-start | bytes 8388608
  312.2 5.0 copy-start.5
  312.2 5.0 slice-start.2
  317.2 2.7 slice-start
  322.7 152.2 %reduce-scatter.9.cloned.1.call-start = ((), (), s32[]{:S(2)}) async-start(), calls=%async_computation.6 | async-start | bytes 3932160 | tf_op jit(solution)/shard_map/reduce_scatter | solution.py:392
  330.0 232.3 %reduce-scatter.13.cloned.1.call-start = ((), (), s32[]{:S(2)}) async-start(), calls=%async_computation.11 | async-start | bytes 5308416
  330.0 4.9 copy-start.3
  330.0 4.9 copy-start.16
  348.6 126.3 %copy-start.2 = (bf16[1,256,1536]{2,1,0:T(8,128)(2,1)S(1)}, bf16[1,256,1536]{2,1,0:T(8,128)(2,1)}, u32[]{:S(2)}) copy-start(bf16[1,256,1536]{2,1,0:T(8,128)(2,1)} %param.16) | copy-start | bytes 2359300
  (5 other events, 8.0 us)
Sparse Core Ops, SparseCore 0:
  9.6 31.2 all-gather.10
  43.6 64.5 all-gather.6
  111.0 78.0 all-gather.8
  190.5 26.8 all-gather.12
  268.4 34.4 all-reduce.1
  310.8 71.9 reduce-scatter.14
  385.4 36.9 reduce-scatter.10
  424.9 37.8 reduce-scatter.8
  466.5 95.7 reduce-scatter.12

commit v2 on v1

--- a/solution.py
+++ b/solution.py
@@ -10,6 +10,7 @@
 WIDTH = 64
 NEG = -1e30
 EPSILON = 1e-05
+MESH = pl.DeviceIdType.MESH
 HIGHEST = lax.Precision.HIGHEST
 F32 = jnp.float32
 BF16 = jnp.bfloat16
@@ -50,10 +51,20 @@
 
 def forward_kernel(
     inner_ref, small_ref, xw_ref, xb_ref, bcw_ref, bcb_ref, bias_ref, alog_ref, skip_ref,
-    y_ref, state_out_ref, xbuf, bcbuf, state, mixed, weighted,
+    pack_ref, rows_ref,
+    y_ref, state_out_ref, all_ref, tokens_ref,
+    xbuf, bcbuf, state, mixed, weighted, ls, lr, ll, qs, qr, ql,
 ):
     step = pl.program_id(0)
     heads = bias_ref.shape[1]
+    line = LineGather(pack_ref, all_ref, ls, lr, ll)
+    quad = QuadGather(rows_ref, tokens_ref, qs, qr, ql)
+
+    @pl.when(step == 0)
+    def _():
+        greet(True, True)
+        line.start()
+        quad.start()
 
     @pl.when(step == 0)
     def _():
@@ -106,12 +117,23 @@
     xbuf[0:8, :] = xbuf[Q : Q + 8, :]
     bcbuf[0:8, :] = bcbuf[Q : Q + 8, :]
 
+    @pl.when(step == pl.num_programs(0) - 1)
+    def _():
+        for hop in range(1, line.nz):
+            line.relay(hop)
+            if hop == 1:
+                quad.relay()
+        quad.finish()
+        line.finish()
+
 
 def full(shape):
     return pl.BlockSpec(shape, lambda i: (0,) * len(shape))
 
 
-def mixer_forward(inner, small, xw, xb, bcw, bcb, bias, alog, skip):
+def mixer_forward(inner, small, xw, xb, bcw, bcb, bias, alog, skip, pack, tokens):
+    n = lax.axis_size("dp")
+    far = pl.BlockSpec(memory_space=pl.ANY)
     rows, channels = inner.shape
     blocks = rows // Q
     wide = small.shape[1]
@@ -124,14 +146,19 @@
             pl.BlockSpec((Q, wide), lambda i: (i, 0)),
             full(xw.shape), full(xb.shape), full(bcw.shape), full(bcb.shape),
             full(bias.shape), full(alog.shape), full(skip.shape),
+            full(pack.shape), full(tokens.shape),
         ],
         out_specs=[
             pl.BlockSpec((Q, channels), lambda i: (i, 0)),
             pl.BlockSpec((1, STATE, channels), lambda i: (i, 0, 0)),
+            far,
+            far,
         ],
         out_shape=[
             jax.ShapeDtypeStruct((rows, channels), F32),
             jax.ShapeDtypeStruct((blocks, STATE, channels), F32),
+            jax.ShapeDtypeStruct((n,) + pack.shape, pack.dtype),
+            jax.ShapeDtypeStruct((4,) + tokens.shape, tokens.dtype),
         ],
         scratch_shapes=[
             pltpu.VMEM((Q + 8, channels), F32),
@@ -139,11 +166,14 @@
             pltpu.VMEM((STATE, channels), F32),
             pltpu.VMEM((1, channels), F32),
             pltpu.VMEM((Q, channels), BF16),
-        ],
+        ]
+        + line_semaphores(n)
+        + quad_semaphores(),
+        compiler_params=pltpu.CompilerParams(collective_id=1, has_side_effects=True),
         cost_estimate=pl.CostEstimate(
             flops=rows * channels * Q * 8, bytes_accessed=rows * channels * 16, transcendentals=rows * channels * 8
         ),
-    )(inner, small, xw, xb, bcw, bcb, bias, alog, skip)
+    )(inner, small, xw, xb, bcw, bcb, bias, alog, skip, pack, tokens)
 
 
 def backward_kernel(
@@ -339,6 +369,194 @@
     )(inner, inner, small, small, gy, states, xw, xb, bcw, bcb, bias, alog, skip)
 
 
+def remote(src, dst, send, recv, **to):
+    return pltpu.make_async_remote_copy(
+        src_ref=src, dst_ref=dst, send_sem=send, recv_sem=recv, device_id=to, device_id_type=MESH
+    )
+
+
+def line_place():
+    me = lax.axis_index("dp")
+    return me // 2, me % 2, lax.axis_size("dp") // 2
+
+
+def quad_place():
+    me = lax.axis_index("tensor")
+    x, core = me // 2, me % 2
+    return me, x * 2 + 1 - core, (1 - x) * 2 + core, (1 - x) * 2 + 1 - core
+
+
+def greet(line, quad):
+    barrier = pltpu.get_barrier_semaphore()
+    count = 0
+    if line:
+        z, y, nz = line_place()
+        pl.semaphore_signal(barrier, inc=1, device_id={"dp": z * 2 + 1 - y}, device_id_type=MESH)
+        count = 1
+
+        @pl.when(z > 0)
+        def _():
+            pl.semaphore_signal(barrier, inc=1, device_id={"dp": z * 2 - 2 + y}, device_id_type=MESH)
+
+        @pl.when(z < nz - 1)
+        def _():
+            pl.semaphore_signal(barrier, inc=1, device_id={"dp": z * 2 + 2 + y}, device_id_type=MESH)
+
+        count = count + jnp.where(z > 0, 1, 0) + jnp.where(z < nz - 1, 1, 0)
+    if quad:
+        _, partner, across, _ = quad_place()
+        pl.semaphore_signal(barrier, inc=1, device_id={"tensor": partner}, device_id_type=MESH)
+        pl.semaphore_signal(barrier, inc=1, device_id={"tensor": across}, device_id_type=MESH)
+        count = count + 2
+    pl.semaphore_wait(barrier, count)
+
+
+class LineGather:
+    def __init__(self, own, out, send, recv, local):
+        self.own, self.out, self.send, self.recv = own, out, send, recv
+        self.z, self.y, self.nz = line_place()
+        self.local = pltpu.make_async_copy(own, out.at[self.z * 2 + self.y], local)
+
+    def copy(self, z, y, way, src=None):
+        slot = z * 2 + y
+        to = (self.z * 2 + 2 + self.y, self.z * 2 - 2 + self.y, self.z * 2 + 1 - self.y)[way]
+        return remote(
+            self.out.at[slot] if src is None else src,
+            self.out.at[slot],
+            self.send.at[slot, way],
+            self.recv.at[slot],
+            dp=to,
+        )
+
+    def each(self, act):
+        z, y, nz = self.z, self.y, self.nz
+        pl.when(z < nz - 1)(lambda: act(self.copy(z, y, 0, self.own)))
+        pl.when(z > 0)(lambda: act(self.copy(z, y, 1, self.own)))
+        act(self.copy(z, y, 2, self.own))
+
+    def start(self):
+        self.each(lambda c: c.start())
+        self.local.start()
+
+    def relay(self, hop):
+        z, y, nz = self.z, self.y, self.nz
+
+        @pl.when(z >= hop)
+        def _():
+            self.copy(z - hop, y, 2).wait_recv()
+            pl.when(z < nz - 1)(lambda: self.copy(z - hop, y, 0).start())
+            self.copy(z - hop, y, 2).start()
+
+        @pl.when(z + hop < nz)
+        def _():
+            self.copy(z + hop, y, 2).wait_recv()
+            pl.when(z > 0)(lambda: self.copy(z + hop, y, 1).start())
+            self.copy(z + hop, y, 2).start()
+
+    def finish(self):
+        z, y, nz = self.z, self.y, self.nz
+        for other in range(nz):
+            self.copy(other, 1 - y, 2).wait_recv()
+        self.local.wait()
+        self.each(lambda c: c.wait_send())
+        for hop in range(1, nz):
+
+            @pl.when(z >= hop)
+            def _():
+                pl.when(z < nz - 1)(lambda: self.copy(z - hop, y, 0).wait_send())
+                self.copy(z - hop, y, 2).wait_send()
+
+            @pl.when(z + hop < nz)
+            def _():
+                pl.when(z > 0)(lambda: self.copy(z + hop, y, 1).wait_send())
+                self.copy(z + hop, y, 2).wait_send()
+
+
+class QuadGather:
+    def __init__(self, own, out, send, recv, local):
+        self.own, self.out, self.send, self.recv = own, out, send, recv
+        self.me, self.partner, self.over, self.diagonal = quad_place()
+        self.local = pltpu.make_async_copy(own, out.at[self.me], local)
+
+    def copy(self, slot, src, way, to):
+        return remote(src, self.out.at[slot], self.send.at[way], self.recv.at[slot], tensor=to)
+
+    def sends(self):
+        return (
+            self.copy(self.me, self.own, 0, self.over),
+            self.copy(self.me, self.own, 1, self.partner),
+            self.copy(self.over, self.out.at[self.over], 2, self.partner),
+        )
+
+    def arrival(self, slot):
+        return self.copy(slot, self.own, 0, self.partner)
+
+    def start(self):
+        across, beside, _ = self.sends()
+        across.start()
+        beside.start()
+        self.local.start()
+
+    def relay(self):
+        self.arrival(self.over).wait_recv()
+        self.sends()[2].start()
+
+    def finish(self):
+        self.arrival(self.partner).wait_recv()
+        self.arrival(self.diagonal).wait_recv()
+        self.local.wait()
+        for send in self.sends():
+            send.wait_send()
+
+
+def line_semaphores(n):
+    return [
+        pltpu.SemaphoreType.DMA((n, 3)),
+        pltpu.SemaphoreType.DMA((n,)),
+        pltpu.SemaphoreType.DMA,
+    ]
+
+
+def quad_semaphores():
+    return [
+        pltpu.SemaphoreType.DMA((3,)),
+        pltpu.SemaphoreType.DMA((4,)),
+        pltpu.SemaphoreType.DMA,
+    ]
+
+
+def first_kernel(pack_ref, rows_ref, all_ref, tokens_ref, ls, lr, ll, qs, qr, ql):
+    greet(True, True)
+    line = LineGather(pack_ref, all_ref, ls, lr, ll)
+    quad = QuadGather(rows_ref, tokens_ref, qs, qr, ql)
+    line.start()
+    quad.start()
+    for hop in range(1, line.nz):
+        line.relay(hop)
+        if hop == 1:
+            quad.relay()
+    quad.finish()
+    line.finish()
+
+
+def gather_first(pack, rows):
+    n = lax.axis_size("dp")
+    whole = pl.BlockSpec(memory_space=pltpu.VMEM)
+    far = pl.BlockSpec(memory_space=pl.ANY)
+    return pl.pallas_call(
+        first_kernel,
+        name="gather_first",
+        in_specs=[whole, whole],
+        out_specs=[far, far],
+        out_shape=[
+            jax.ShapeDtypeStruct((n,) + pack.shape, pack.dtype),
+            jax.ShapeDtypeStruct((4,) + rows.shape, rows.dtype),
+        ],
+        scratch_shapes=line_semaphores(n) + quad_semaphores(),
+        compiler_params=pltpu.CompilerParams(collective_id=0, has_side_effects=True),
+    )(pack, rows)
+
+
 def local(
     hidden_in, d_out, in_gain, w_zx, w_dt, w_bc, w_out,
     conv_x_w, conv_x_b, conv_bc_w, conv_bc_b, dt_bias, a_log, d_skip, norm_scale,
@@ -348,16 +566,16 @@
     heads = w_dt.shape[1]
     tensor_index = lax.axis_index("tensor")
     parts = lax.axis_size("tensor")
-    hidden_bf = lax.all_gather(hidden_in[0], "tensor", axis=0, tiled=True)
-    first_pack = jnp.concatenate([w_zx[:, 1, :], w_bc, w_dt, in_gain[:, None]], 1)
-    first = lax.all_gather(first_pack, "dp", axis=0, tiled=True)
+    own_width = in_gain.shape[0]
+    spare = jnp.zeros((own_width, 127 - heads), BF16)
+    first_pack = jnp.concatenate([w_zx[:, 1, :], w_bc, w_dt, in_gain[:, None], spare], 1)
+    first, hidden_bf = gather_first(first_pack, hidden_in[0])
+    first = first.reshape(width, -1)
+    hidden_bf = hidden_bf.reshape(-1, width)
     second_pack = jnp.concatenate([w_zx[:, 0, :], w_out], 1)
-    second = lax.all_gather(second_pack, "dp", axis=0, tiled=True)
-    dout_all = lax.all_gather(d_out[0], "tensor", axis=0, tiled=True)
     w_inner = first[:, :inner_local]
     w_small = first[:, inner_local : inner_local + 2 * STATE + heads]
-    gain = first[:, -1].astype(F32)[None]
-    w_gate, w_o = second[:, :inner_local], second[:, inner_local:]
+    gain = first[:, inner_local + 2 * STATE + heads].astype(F32)[None]
 
     hidden = hidden_bf.astype(F32)
     rh = lax.rsqrt(jnp.mean(hidden * hidden, axis=-1, keepdims=True) + EPSILON)
@@ -367,7 +585,10 @@
     params = (
         conv_x_w, conv_x_b[None], conv_bc_w, conv_bc_b[None], dt_bias[None], a_log[None], d_skip[None],
     )
-    y, states = mixer_forward(inner, small, *params)
+    y, states, second, dout_all = mixer_forward(inner, small, *params, second_pack, d_out[0])
+    second = second.reshape(width, -1)
+    dout_all = dout_all.reshape(-1, width)
+    w_gate, w_o = second[:, :inner_local], second[:, inner_local:]
     gate = dot(xn, w_gate)
     dyn = dot(dout_all, w_o)
     sig = jax.nn.sigmoid(gate)

time: 574 us -> 492 us (0.86)
  waiting for transfers between devices: 357 us -> 182 us
  Pallas kernels: 40.8 us -> 132 us
  local copies, waits for them, and re-layouts: 24.7 us -> 31.9 us
  matrix products: 56.6 us -> 49.7 us
    all_gather x4 -> x0, waiting for transfers between devices: 171 us -> none  [the longest x1 64.7 us: local(): first = lax.all_gather(first_pack, 'dp', axis=0, tiled=True)]
    pallas_call x0 -> x1, Pallas kernels: none -> 48 us  [gather_first(): pl.pallas_call(first_kernel, name='gather_first', in_specs=[whole, whole]...]
    pallas_call x1, Pallas kernels: 13.4 us -> 56.8 us  [mixer_forward(): pl.pallas_call(forward_kernel, name='mixer_forward', grid=(blocks,), in_s...]
    dot_general x11, matrix products: 56.6 us -> 49.7 us  [dot(): lax.dot_general(a, b, (dims, ((), ())), precision=precision, preferred_el...]
    unnamed x11 -> x7, waiting for transfers between devices: 119 us -> 115 us
    unnamed x51 -> x63, local copies, waits for them, and re-layouts: 13.8 us -> 17.4 us
  transfers between devices with their start and end apart: 9 -> 5, of which waited for: 8 -> 4; matrix products, arithmetic and copies ran while one was open for 12% -> 10% of each run, Pallas kernels for 2% -> 0%
where the time goes in v2:
time: 492 us; the launch traced here: 491 us
  waiting for transfers between devices  182 us (37%)
  Pallas kernels  132 us (27%)
  blocking collectives  61.1 us (12%)
  matrix products  49.7 us (10%)
  local copies, waits for them, and re-layouts  31.9 us (6%)
  other arithmetic  19.6 us (4%)
  between operations  14.3 us (3%)
    unnamed x7, waiting for transfers between devices  115 us
    pallas_call x1, Pallas kernels, mixer_forward(): pl.pallas_call(forward_kernel, name='mixer_forward', grid=(blocks,), in_s...  56.8 us
    dot_general x11, matrix products, dot(): lax.dot_general(a, b, (dims, ((), ())), precision=precision, preferred_el...  49.7 us
    pallas_call x1, Pallas kernels, gather_first(): pl.pallas_call(first_kernel, name='gather_first', in_specs=[whole, whole]...  48 us
    psum x1, blocking collectives, local(): flat = lax.psum(flat, 'dp')  37.1 us
    psum x1, waiting for transfers between devices, local(): d_bc_low = lax.psum(d_bc, 'tensor')  35.2 us
    reduce_scatter x1, waiting for transfers between devices, local(): lax.psum_scatter(low(d_xn), 'tensor', scatter_dimension=0, tiled=True)  31.1 us
    pallas_call x1, Pallas kernels, mixer_backward(): pl.pallas_call(backward_kernel, name='mixer_backward', grid=(blocks,), in...  27.4 us
  transfers between devices with their start and end apart: 5, of which 4 were waited for; matrix products, arithmetic and copies ran while one was open for 10% of the time, Pallas kernels for 0%

profile of v2, /device:TPU:0, one launch (start us, length us, event | category | flops | bytes accessed | tf_op | source)
XLA Modules:
  0.0 490.9 jit_solution(10300642884480891968)
XLA Ops:
  12.9 48.0 %gather_first.1 = (bf16[8,192,1152]{2,1,0:T(8,128)(2,1)}, bf16[4,256,1536]{2,1,0:T(8,128)(2,1)}) custom-call(bf16[192,1152]{1,0:T(8,128)(2,1)} %concatenate.21.pack_ref, bf16[256,1536]{1,0:T(8,128)(2,1)} %bitcast.52), custom_call_target="tpu_custom_call" | custom-call | tf_op jit(solution)/shard_map/gather_first/pallas_call | solution.py:546
  67.1 2.9 fusion.31.small_ref.sprev_ref
  70.0 4.2 fusion.12.inner_ref.prev_ref
  75.7 56.8 %mixer_forward.1 = (f32[1024,768]{1,0:T(8,128)}, f32[8,128,768]{2,1,0:T(8,128)}, bf16[8,192,1536]{2,1,0:T(8,128)(2,1)}, bf16[4,256,1536]{2,1,0:T(8,128)(2,1)}) custom-call(f32[1024,768]{1,0:T(8,128)} %fusion.12.inner_ref.prev_ref, f32[1024,268]{1,0:T(8,128)} %fusion.31.small_ref.sprev_ref, f32[4,768]{1,0:T(4,128)} %xw_ref.3, ...), custom_call_target="tpu_custom_call" | custom-call | flops 805306368 | bytes 12582912 | tf_op jit(solution)/shard_map/mixer_forward/pallas_call | solution.py:140
  132.5 4.4 fusion.8
  137.4 5.0 %multiply_reduce_fusion.3 = (f32[1024]{0:T(1024)S(1)}, f32[1024]{0:T(1024)S(1)}, f32[1024,768]{1,0:T(8,128)}, f32[1024,768]{1,0:T(8,128)}) fusion(f32[768]{0:T(1024)S(1)} %copy-done.19, f32[1024,768]{1,0:T(8,128)S(1)} %copy-done.5, f32[1024,768]{1,0:T(8,128)S(1)} %fusion.8, bf16[1024,1536]{1,0:T(8,128)(2,1)S(1)} %bitcast.80, bf16[1536,1536]{1,0:T(8,128)(2,1)S(1)} %bitcast.79), kind=kOutput, calls=%fused_computation.15 | convolution fusion | flops 2423781376 | bytes 18100224 | tf_op jit(solution)/shard_map/dot_general | solution.py:20
  142.4 8.0 %psum.28 = f32[2,1024]{1,0:T(2,128)S(1)} all-reduce(f32[2,1024]{1,0:T(2,128)S(1)} %pad_maximum_fusion.3), channel_id=1, replica_groups=mesh['dp'=8,'tensor'=4] {'tensor'}, use_global_device_ids=true, to_apply=%region_3.0 | all-reduce | flops 2048 | bytes 16384 | tf_op jit(solution)/shard_map/psum | solution.py:599
  150.5 7.2 %fusion.30 = (f32[1024,768]{1,0:T(8,128)}, bf16[1024,768]{1,0:T(8,128)(2,1)}, f32[768]{0:T(1024)S(1)}) fusion(f32[1024]{0:T(1024)S(1)} %bitcast.65, f32[1024,768]{1,0:T(8,128)} %get-tuple-element.88, f32[1024,768]{1,0:T(8,128)} %get-tuple-element.105, f32[1024]{0:T(1024)S(1)} %multiply_multiply_fusion, f32[1024]{0:T(1024)S(1)} %bitcast.61, ...), kind=kLoop, calls=%fused_computation.52 | loop fusion | flops 16514304 | bytes 17319936 | tf_op jit(solution)/shard_map/mul | solution.py:605
  157.8 27.4 %mixer_backward.1 = (bf16[1024,768]{1,0:T(8,128)(2,1)}, bf16[1024,12]{1,0:T(8,128)(2,1)}, bf16[1024,256]{1,0:T(8,128)(2,1)}, f32[5,768]{1,0:T(8,128)}, f32[5,256]{1,0:T(8,128)}, /*index=5*/f32[3,12]{1,0:T(4,128)}) custom-call(f32[1024,768]{1,0:T(8,128)} %fusion.12.inner_ref.prev_ref, f32[1024,768]{1,0:T(8,128)} %fusion.12.inner_ref.prev_ref, ...), custom_call_target="tpu_custom_call" | custom-call | flops 2013265920 | bytes 15728640 | tf_op jit(solution)/shard_map/mixer_backward/pallas_call | solution.py:324
  185.3 35.2 %all-reduce.2.cloned.1.call-done = bf16[1024,256]{1,0:T(8,128)(2,1)} async-done(((bf16[1024,256]{1,0:T(8,128)(2,1)}), bf16[1024,256]{1,0:T(8,128)(2,1)}) %all-reduce.2.cloned.1.call-update) | async-done | bytes 524304 | tf_op jit(solution)/shard_map/psum | solution.py:620
  222.3 6.5 %convolution_convert_fusion.1 = bf16[1536,844]{1,0:T(8,128)(2,1)} fusion(bf16[1024,1536]{1,0:T(8,128)(2,1)S(1)} %copy-done.3, bf16[1024,12]{1,0:T(8,128)(2,1)} %get-tuple-element.35, bf16[1024,64]{1,0:T(8,128)(2,1)S(1)} %constant_dynamic-slice_fusion.1, bf16[1024,768]{1,0:T(8,128)(2,1)} %get-tuple-element.33), kind=kOutput, calls=%fused_computation.7 | convolution fusion | flops 2661476352 | bytes 7467008 | tf_op jit(solution)/shard_map/dot_general | solution.py:20
  231.1 4.9 fusion.10
  236.0 4.4 fusion.6
  243.9 6.9 %convolution_convert_fusion = bf16[1024,1536]{1,0:T(8,128)(2,1)} fusion(bf16[1536,1536]{1,0:T(8,128)(2,1)} %bitcast.78, f32[1024,768]{1,0:T(8,128)} %get-tuple-element.88, f32[1024]{0:T(1024)S(1)} %bitcast.62, f32[768]{0:T(1024)S(1)} %copy-done.20), kind=kOutput, calls=%fused_computation.6 | convolution fusion | flops 2419851264 | bytes 8657920 | tf_op jit(solution)/shard_map/dot_general | solution.py:20
  250.9 4.6 convolution_convert_fusion.3
  255.5 3.1 convolution_convert_fusion.2
  261.0 6.7 %copy.75 = bf16[1536,1536]{1,0:T(8,128)(2,1)} copy(bf16[1536,1536]{0,1:T(8,128)(2,1)} %pad_maximum_fusion) | data formatting | bytes 9437184
  269.1 31.9 %reduce-scatter.15.cloned.1.call-done = bf16[192,844]{1,0:T(8,128)(2,1)} async-done(((bf16[1536,844]{1,0:T(8,128)(2,1)}), bf16[192,844]{1,0:T(8,128)(2,1)}) %reduce-scatter.15.cloned.1.call-update) | async-done | bytes 324112
  302.9 5.8 %all_gather.3 = f32[192,256]{0,1:T(8,128)S(1)} all-gather(f32[192,64]{0,1:T(8,128)S(1)} %slice.149), channel_id=1, replica_groups=mesh['dp'=8,'tensor'=4] {'tensor'}, dimensions={1}, use_global_device_ids=true | all-gather | bytes 245760 | tf_op jit(solution)/shard_map/all_gather | solution.py:655
  309.5 31.1 %reduce-scatter.11.cloned.1.call-done = bf16[256,1536]{1,0:T(8,128)(2,1)} async-done(((bf16[1024,1536]{1,0:T(8,128)(2,1)}), bf16[256,1536]{1,0:T(8,128)(2,1)}) %reduce-scatter.11.cloned.1.call-update) | async-done | bytes 786448 | tf_op jit(solution)/shard_map/reduce_scatter | solution.py:635
  342.2 37.1 %psum.30 = f32[7460]{0:T(1024)S(1)} all-reduce(f32[7460]{0:T(1024)S(1)} %constant_dynamic-update-slice_fusion), channel_id=1, replica_groups=mesh['dp'=8,'tensor'=4] {'dp'}, use_global_device_ids=true, to_apply=%region_11.0 | all-reduce | flops 7460 | bytes 59680 | tf_op jit(solution)/shard_map/psum | solution.py:646
  379.3 10.2 %psum.31 = f32[2816]{0:T(1024)S(1)} all-reduce(f32[2816]{0:T(1024)S(1)} %slice.145), channel_id=1, replica_groups=mesh['dp'=8,'tensor'=4] {'tensor'}, use_global_device_ids=true, to_apply=%region_12.0 | all-reduce | flops 2816 | bytes 22528 | tf_op jit(solution)/shard_map/psum | solution.py:648
  393.2 3.5 fusion.22
  396.6 83.6 %reduce-scatter.13.cloned.1.call-done = bf16[192,1536]{1,0:T(8,128)(2,1)} async-done(((bf16[1536,1536]{1,0:T(8,128)(2,1)}), bf16[192,1536]{1,0:T(8,128)(2,1)}) %reduce-scatter.13.cloned.1.call-update) | async-done | bytes 589840
  (118 shorter events, 37.4 us)
Async XLA Ops:
  7.2 4.9 copy-start.15
  7.2 213.3 %all-reduce.2.cloned.1.call-start = ((), (), s32[]{:S(2)}) async-start(), calls=%async_computation.5 | async-start | bytes 1048576 | tf_op jit(solution)/shard_map/psum | solution.py:620
  60.9 4.1 copy-start
  65.1 2.0 copy-start.12
  67.1 2.9 copy-start.2
  70.0 4.2 copy-start.18
  70.0 4.8 copy-start.8
  70.0 4.8 copy-start.13
  75.7 56.8 %copy-start.3 = (bf16[1024,1536]{1,0:T(8,128)(2,1)S(1)}, bf16[1024,1536]{1,0:T(8,128)(2,1)}, u32[]{:S(2)}) copy-start(bf16[1024,1536]{1,0:T(8,128)(2,1)} %copy-done.2) | copy-start | bytes 9437188
  132.5 4.5 copy-start.5
  132.5 4.5 copy-start.19
  132.5 4.5 copy-start.22
  132.5 4.9 copy-start.23
  136.9 5.5 %copy-start.6 = (f32[1024,768]{1,0:T(8,128)}, f32[1024,768]{1,0:T(8,128)S(1)}, u32[]{:S(2)}) copy-start(f32[1024,768]{1,0:T(8,128)S(1)} %fusion.8) | copy-start | bytes 9437188
  185.2 115.8 %reduce-scatter.15.cloned.1.call-start = ((), (), s32[]{:S(2)}) async-start(), calls=%async_computation.8 | async-start | bytes 3096576
  228.8 111.8 %reduce-scatter.11.cloned.1.call-start = ((), (), s32[]{:S(2)}) async-start(), calls=%async_computation.6 | async-start | bytes 3932160 | tf_op jit(solution)/shard_map/reduce_scatter | solution.py:635
  231.0 4.9 copy-start.7
  236.0 4.4 copy-start.10
  236.0 4.4 copy-start.14
  243.2 149.9 %reduce-scatter.9.cloned.1.call-start = ((), (), s32[]{:S(2)}) async-start(), calls=%async_computation.4 | async-start | bytes 3932160 | tf_op jit(solution)/shard_map/reduce_scatter | solution.py:613
  250.9 229.3 %reduce-scatter.13.cloned.1.call-start = ((), (), s32[]{:S(2)}) async-start(), calls=%async_computation.7 | async-start | bytes 5308416
  250.9 4.6 copy-start.4
  250.9 4.6 copy-start.24
  269.1 124.0 %copy-start.11 = (bf16[1,256,1536]{2,1,0:T(8,128)(2,1)S(1)}, bf16[1,256,1536]{2,1,0:T(8,128)(2,1)}, u32[]{:S(2)}) copy-start(bf16[1,256,1536]{2,1,0:T(8,128)(2,1)} %param.16) | copy-start | bytes 2359300
  (6 other events, 4.8 us)
Sparse Core Ops, SparseCore 0:
  185.3 35.0 all-reduce.1
  228.9 72.0 reduce-scatter.14
  303.5 36.9 reduce-scatter.10
  343.0 37.8 reduce-scatter.8
  384.4 95.7 reduce-scatter.12

commit v3 on v2

--- a/solution.py
+++ b/solution.py
@@ -179,11 +179,32 @@
 def backward_kernel(
     inner_ref, prev_ref, small_ref, sprev_ref, gy_ref, state_ref,
     xw_ref, xb_ref, bcw_ref, bcb_ref, bias_ref, alog_ref, skip_ref,
-    dinner_ref, ddt_ref, dbc_ref, gxw_ref, gbcw_ref, ghead_ref,
+    gate_grad_ref, out_grad_ref, branch_part_ref,
+    dinner_ref, ddt_ref, dbc_ref, grads_ref, gate_sum_ref, out_sum_ref, branch_ref,
     xbuf, bcbuf, dxbuf, dbcbuf, dstate, carried, back, rows_buf, sums, cgy, weighted, decay_row,
+    dbc_mine, dbc_there, bsend, brecv, *scratch,
 ):
     step = pl.program_id(0)
     blocks = pl.num_programs(0)
+    me, partner, over, diagonal = quad_place()
+    gate_scatter = LineScatter(gate_grad_ref, gate_sum_ref, *scratch[0:5])
+    out_scatter = LineScatter(out_grad_ref, out_sum_ref, *scratch[5:10])
+    branch = QuadScatter(branch_part_ref, branch_ref, *scratch[10:14])
+    hops = list(range(out_scatter.nz - 1, 0, -1))
+    rounds = [(stream, hop) for hop in hops for stream in (out_scatter, gate_scatter)]
+    own_columns = 2 * STATE // 4
+
+    def column_copies(block):
+        def copy(way, to):
+            return remote(
+                dbc_mine.at[block, pl.ds(pl.multiple_of(to * own_columns, own_columns), own_columns), :],
+                dbc_there.at[way, block],
+                bsend.at[way, block],
+                brecv.at[way, block],
+                tensor=to,
+            )
+
+        return copy(0, partner), copy(1, over), copy(2, diagonal)
     heads = bias_ref.shape[1]
     channels = inner_ref.shape[1]
 
@@ -192,9 +213,17 @@
         dstate[...] = jnp.zeros_like(dstate)
         dxbuf[Q:, :] = jnp.zeros((8, channels), F32)
         dbcbuf[Q:, :] = jnp.zeros((8, 2 * STATE), F32)
-        gxw_ref[...] = jnp.zeros_like(gxw_ref)
-        gbcw_ref[...] = jnp.zeros_like(gbcw_ref)
-        ghead_ref[...] = jnp.zeros_like(ghead_ref)
+        grads_ref[...] = jnp.zeros_like(grads_ref)
+        greet(True, True)
+        for hop in hops + [0]:
+            out_scatter.open(hop)
+            gate_scatter.open(hop)
+        branch.start()
+
+    pl.when(step == 1)(lambda: branch.middle())
+    early_rounds = {2: rounds[0], 4: rounds[1], 6: rounds[2]}
+    for at_step, (stream, hop) in early_rounds.items():
+        pl.when(step == at_step)(lambda: stream.round(hop))
 
     first = step == blocks - 1
     xbuf[0:8, :] = jnp.where(first, 0.0, prev_ref[...])
@@ -277,8 +306,8 @@
             out = out + xw[k : k + 1, sl] * dxbuf[pl.ds(3 - k, Q), sl]
         dinner_ref[:, sl] = low(out)
         for k in range(4):
-            gxw_ref[k : k + 1, sl] += jnp.sum(dpre * shifted[k], axis=0, keepdims=True)
-        gxw_ref[4:5, sl] += jnp.sum(dpre, axis=0, keepdims=True)
+            grads_ref[8 + k : 9 + k, sl] += jnp.sum(dpre * shifted[k], axis=0, keepdims=True)
+        grads_ref[12:13, sl] += jnp.sum(dpre, axis=0, keepdims=True)
     head_of = lax.broadcasted_iota(jnp.int32, (channels, heads), 0) // WIDTH
     head = lax.broadcasted_iota(jnp.int32, (channels, heads), 1)
     head_hot = (head_of == head).astype(BF16)
@@ -292,9 +321,9 @@
     ddecay = dot(causal_t.astype(F32), dcum, precision=HIGHEST) + dlast
     ddt = (ddecay * a + t_x) * jax.nn.sigmoid(raw)
     ddt_ref[...] = low(ddt)
-    ghead_ref[0:1, :] += jnp.sum(ddt, axis=0, keepdims=True)
-    ghead_ref[1:2, :] += jnp.sum(ddecay * dt, axis=0, keepdims=True) * a
-    ghead_ref[2:3, :] += jnp.sum(t_skip, axis=0, keepdims=True)
+    grads_ref[4:5, 0:heads] += jnp.sum(ddt, axis=0, keepdims=True)
+    grads_ref[5:6, 0:heads] += jnp.sum(ddecay * dt, axis=0, keepdims=True) * a
+    grads_ref[6:7, 0:heads] += jnp.sum(t_skip, axis=0, keepdims=True)
     dsl = low(dscores_t)
     dc = dot(dsl, b, ((0,), (0,))) + dot(cgy[...], state_low, ((1,), (1,)))
     db = dot(dsl, c) + dot(weighted[...], dstate_low, ((1,), (1,)))
@@ -306,15 +335,42 @@
     out = bcw[3:4] * dpre
     for k in range(3):
         out = out + bcw[k : k + 1] * dbcbuf[pl.ds(3 - k, Q), :]
-    dbc_ref[...] = out.astype(dbc_ref.dtype)
+    block = blocks - 1 - step
+    dbc_mine[block] = low(out.T)
+    for copy in column_copies(block):
+        copy.start()
     for k in range(4):
-        gbcw_ref[k : k + 1, :] += jnp.sum(dpre * bcbuf[pl.ds(5 + k, Q), :], axis=0, keepdims=True)
-    gbcw_ref[4:5, :] += jnp.sum(dpre, axis=0, keepdims=True)
+        part = jnp.sum(dpre * bcbuf[pl.ds(5 + k, Q), :], axis=0, keepdims=True)
+        at = 2 * STATE * (k % 3)
+        grads_ref[2 + k // 3 : 3 + k // 3, at : at + 2 * STATE] += part
+    grads_ref[3:4, 2 * STATE : 4 * STATE] += jnp.sum(dpre, axis=0, keepdims=True)
     dxbuf[Q:, :] = dxbuf[0:8, :]
     dbcbuf[Q:, :] = dbcbuf[0:8, :]
 
-
-def mixer_backward(inner, small, gy, states, xw, xb, bcw, bcb, bias, alog, skip, dbc_dtype=F32):
+    @pl.when(step == blocks - 1)
+    def _():
+        for i in range(dbc_mine.shape[0]):
+            for copy in column_copies(i):
+                copy.wait_recv()
+            mine = dbc_mine[i, pl.ds(pl.multiple_of(me * own_columns, own_columns), own_columns), :]
+            total = mine.astype(F32)
+            for way in range(3):
+                total = total + dbc_there[way, i].astype(F32)
+            dbc_ref[:, i * Q : (i + 1) * Q] = low(total)
+        branch.finish()
+        for stream, hop in rounds[3:]:
+            stream.round(hop)
+        out_scatter.finish()
+        gate_scatter.finish()
+        for i in range(dbc_mine.shape[0]):
+            for copy in column_copies(i):
+                copy.wait_send()
+
+
+def mixer_backward(inner, small, gy, states, xw, xb, bcw, bcb, bias, alog, skip, gate_grad, out_grad, branch):
+    n, share, side = gate_grad.shape
+    tokens, features = branch.shape[1:]
+    far = pl.BlockSpec(memory_space=pl.ANY)
     rows, channels = inner.shape
     blocks = rows // Q
     wide = small.shape[1]
@@ -334,20 +390,22 @@
             pl.BlockSpec((1, STATE, channels), lambda i: (at(i), 0, 0)),
             full(xw.shape), full(xb.shape), full(bcw.shape), full(bcb.shape),
             full(bias.shape), full(alog.shape), full(skip.shape),
+            far, far, far,
         ],
         out_specs=[
             pl.BlockSpec((Q, channels), lambda i: (at(i), 0)),
             pl.BlockSpec((Q, heads), lambda i: (at(i), 0)),
-            pl.BlockSpec((Q, 2 * STATE), lambda i: (at(i), 0)),
-            full((5, channels)), full((5, 2 * STATE)), full((3, heads)),
+            full((2 * STATE // 4, rows)),
+            full((16, channels)), full((share, side)), full((share, side)), full((tokens, features)),
         ],
         out_shape=[
             jax.ShapeDtypeStruct((rows, channels), BF16),
             jax.ShapeDtypeStruct((rows, heads), BF16),
-            jax.ShapeDtypeStruct((rows, 2 * STATE), dbc_dtype),
-            jax.ShapeDtypeStruct((5, channels), F32),
-            jax.ShapeDtypeStruct((5, 2 * STATE), F32),
-            jax.ShapeDtypeStruct((3, heads), F32),
+            jax.ShapeDtypeStruct((2 * STATE // 4, rows), BF16),
+            jax.ShapeDtypeStruct((16, channels), F32),
+            jax.ShapeDtypeStruct((share, side), F32),
+            jax.ShapeDtypeStruct((share, side), F32),
+            jax.ShapeDtypeStruct((tokens, features), F32),
         ],
         scratch_shapes=[
             pltpu.VMEM((Q + 8, channels), F32),
@@ -362,11 +420,19 @@
             pltpu.VMEM((Q, channels), BF16),
             pltpu.VMEM((Q, channels), BF16),
             pltpu.VMEM((1, channels), F32),
-        ],
+            pltpu.VMEM((blocks, 2 * STATE, Q), BF16),
+            pltpu.VMEM((3, blocks, 2 * STATE // 4, Q), BF16),
+            pltpu.SemaphoreType.DMA((3, blocks)),
+            pltpu.SemaphoreType.DMA((3, blocks)),
+        ]
+        + line_scatter_scratch(n, share, side)
+        + line_scatter_scratch(n, share, side)
+        + quad_scatter_scratch(tokens, features),
+        compiler_params=pltpu.CompilerParams(collective_id=2, has_side_effects=True),
         cost_estimate=pl.CostEstimate(
             flops=rows * channels * Q * 20, bytes_accessed=rows * channels * 20, transcendentals=rows * channels * 10
         ),
-    )(inner, inner, small, small, gy, states, xw, xb, bcw, bcb, bias, alog, skip)
+    )(inner, inner, small, small, gy, states, xw, xb, bcw, bcb, bias, alog, skip, gate_grad, out_grad, branch)
 
 
 def remote(src, dst, send, recv, **to):
@@ -404,10 +470,9 @@
 
         count = count + jnp.where(z > 0, 1, 0) + jnp.where(z < nz - 1, 1, 0)
     if quad:
-        _, partner, across, _ = quad_place()
-        pl.semaphore_signal(barrier, inc=1, device_id={"tensor": partner}, device_id_type=MESH)
-        pl.semaphore_signal(barrier, inc=1, device_id={"tensor": across}, device_id_type=MESH)
-        count = count + 2
+        for other in quad_place()[1:]:
+            pl.semaphore_signal(barrier, inc=1, device_id={"tensor": other}, device_id_type=MESH)
+        count = count + 3
     pl.semaphore_wait(barrier, count)
 
 
@@ -555,6 +620,311 @@
         scratch_shapes=line_semaphores(n) + quad_semaphores(),
         compiler_params=pltpu.CompilerParams(collective_id=0, has_side_effects=True),
     )(pack, rows)
+
+
+def add_rows(target, *sources):
+    rows = target.shape[0]
+    group = 48 if rows % 48 == 0 else 32
+
+    @pl.loop(0, rows // group)
+    def _(i):
+        at = pl.ds(pl.multiple_of(i * group, 16), group)
+        total = sources[0][at, :].astype(F32)
+        for source in sources[1:]:
+            total = total + source[at, :].astype(F32)
+        target[at, :] = total.astype(target.dtype)
+
+
+class LineScatter:
+    def __init__(self, src, out, mine, near, below, above, sems):
+        self.src, self.out, self.mine, self.near = src, out, mine, near
+        self.below, self.above, self.sems = below, above, sems
+        self.z, self.y, self.nz = line_place()
+
+    def load(self, t):
+        return pltpu.make_async_copy(
+            self.src.at[t * 2 + self.y], self.mine.at[t], self.sems.at[0, t]
+        )
+
+    def beside(self, t):
+        other = 1 - self.y
+        return remote(
+            self.src.at[t * 2 + other], self.near.at[t], self.sems.at[1, t], self.sems.at[2, t],
+            dp=self.z * 2 + other,
+        )
+
+    def up(self, t):
+        return remote(
+            self.near.at[t], self.below.at[t], self.sems.at[3, t], self.sems.at[4, t],
+            dp=self.z * 2 + 2 + self.y,
+        )
+
+    def down(self, t):
+        return remote(
+            self.near.at[t], self.above.at[t], self.sems.at[3, t], self.sems.at[5, t],
+            dp=self.z * 2 - 2 + self.y,
+        )
+
+    def open(self, hop):
+        z, nz = self.z, self.nz
+
+        def begin(t):
+            self.beside(t).start()
+            self.load(t).start()
+
+        if hop == 0:
+            begin(z)
+        else:
+            pl.when(z + hop < nz)(lambda: begin(z + hop))
+            pl.when(z >= hop)(lambda: begin(z - hop))
+
+    def round(self, hop):
+        z, nz = self.z, self.nz
+
+        def ready(t):
+            self.load(t).wait()
+            self.beside(t).wait_recv()
+
+        @pl.when(z + hop < nz)
+        def _():
+            t = z + hop
+            ready(t)
+
+            @pl.when(z > 0)
+            def _():
+                self.up(t).wait_recv()
+                add_rows(self.near.at[t], self.mine.at[t], self.near.at[t], self.below.at[t])
+
+            @pl.when(z == 0)
+            def _():
+                add_rows(self.near.at[t], self.mine.at[t], self.near.at[t])
+
+            self.up(t).start()
+
+        @pl.when(z >= hop)
+        def _():
+            t = z - hop
+            ready(t)
+
+            @pl.when(z < nz - 1)
+            def _():
+                self.down(t).wait_recv()
+                add_rows(self.near.at[t], self.mine.at[t], self.near.at[t], self.above.at[t])
+
+            @pl.when(z == nz - 1)
+            def _():
+                add_rows(self.near.at[t], self.mine.at[t], self.near.at[t])
+
+            self.down(t).start()
+
+    def finish(self):
+        z, nz = self.z, self.nz
+        self.load(z).wait()
+        self.beside(z).wait_recv()
+        pl.when(z > 0)(lambda: self.up(z).wait_recv())
+        pl.when(z < nz - 1)(lambda: self.down(z).wait_recv())
+        own = (self.mine.at[z], self.near.at[z])
+
+        @pl.when(z == 0)
+        def _():
+            add_rows(self.out, *own, self.above.at[z])
+
+        @pl.when(z == nz - 1)
+        def _():
+            add_rows(self.out, *own, self.below.at[z])
+
+        @pl.when((z > 0) & (z < nz - 1))
+        def _():
+            add_rows(self.out, *own, self.below.at[z], self.above.at[z])
+
+        for t in range(nz):
+            self.beside(t).wait_send()
+            pl.when(z < t)(lambda: self.up(t).wait_send())
+            pl.when(z > t)(lambda: self.down(t).wait_send())
+
+
+class QuadScatter:
+    def __init__(self, src, out, mine, side, far, sems):
+        self.src, self.out, self.mine, self.side, self.far = src, out, mine, side, far
+        self.sems = sems
+        self.me, self.partner, self.over, self.diagonal = quad_place()
+
+    def copies(self):
+        return (
+            pltpu.make_async_copy(self.src.at[self.me], self.mine.at[0], self.sems.at[0]),
+            pltpu.make_async_copy(self.src.at[self.over], self.mine.at[1], self.sems.at[1]),
+            remote(
+                self.src.at[self.diagonal], self.side.at[1], self.sems.at[2], self.sems.at[3],
+                tensor=self.partner,
+            ),
+            remote(
+                self.src.at[self.partner], self.side.at[0], self.sems.at[4], self.sems.at[5],
+                tensor=self.partner,
+            ),
+            remote(self.side.at[1], self.far, self.sems.at[6], self.sems.at[7], tensor=self.over),
+        )
+
+    def start(self):
+        own, passing, first, second, _ = self.copies()
+        first.start()
+        passing.start()
+        second.start()
+        own.start()
+
+    def middle(self):
+        _, passing, first, _, across = self.copies()
+        passing.wait()
+        first.wait_recv()
+        add_rows(self.side.at[1], self.mine.at[1], self.side.at[1])
+        across.start()
+
+    def finish(self):
+        own, _, first, second, across = self.copies()
+        own.wait()
+        second.wait_recv()
+        across.wait_recv()
+        if self.out is not None:
+            add_rows(self.out, self.mine.at[0], self.side.at[0], self.far)
+        first.wait_send()
+        second.wait_send()
+        across.wait_send()
+
+
+def line_scatter_scratch(n, rows, columns):
+    return [pltpu.VMEM((n // 2, rows, columns), BF16)] * 4 + [pltpu.SemaphoreType.DMA((6, n // 2))]
+
+
+def quad_scatter_scratch(rows, columns):
+    return [
+        pltpu.VMEM((2, rows, columns), BF16),
+        pltpu.VMEM((2, rows, columns), BF16),
+        pltpu.VMEM((rows, columns), BF16),
+        pltpu.SemaphoreType.DMA((8,)),
+    ]
+
+
+def last_kernel(
+    small_ref, one_ref, two_ref, dx_ref, hidden_ref, dout_ref, gain_ref, mix_ref, scale_ref,
+    d_hidden_ref, bc_ref, dt_ref, left_ref, right_ref, flat_ref, shared_ref,
+    *scratch,
+):
+    s0, s1, s2 = scratch[0:5], scratch[5:10], scratch[10:15]
+    quad_scratch = scratch[15:19]
+    flat, flat_all, shared_own, shared_all, small_sum, bc_all = scratch[19:25]
+    ls, lr, ll, qs, qr, ql, bs, br, bl = scratch[25:34]
+    greet(True, True)
+    small = LineScatter(small_ref, small_sum, *s0)
+    one = LineScatter(one_ref, left_ref, *s1)
+    two = LineScatter(two_ref, right_ref, *s2)
+    dx = QuadScatter(dx_ref, None, *quad_scratch)
+    hops = list(range(one.nz - 1, 0, -1))
+    for hop in hops + [0]:
+        small.open(hop)
+    dx.start()
+    for hop in hops + [0]:
+        one.open(hop)
+        two.open(hop)
+    dx.middle()
+    for hop in hops:
+        small.round(hop)
+    small.finish()
+    width = small_sum.shape[1]
+    columns = QuadGather(small_sum, bc_all, bs, br, bl)
+    columns.start()
+    middle = max(len(hops) - 1, 1)
+    for i, hop in enumerate(hops):
+        one.round(hop)
+        two.round(hop)
+        if i == 0:
+            columns.relay()
+    dx.finish()
+    mine, side, far = quad_scratch[0].at[0], quad_scratch[1].at[0], quad_scratch[2]
+    flat[...] = mix_ref[...]
+    flat[7:8, :] = scale_ref[...]
+    half = flat.shape[1]
+    features = hidden_ref.shape[1]
+    group = 32
+
+    def token_rows(i, total):
+        at = pl.ds(pl.multiple_of(i * group, group), group)
+        d_normed = mine[at, :].astype(F32) + side[at, :].astype(F32) + far[at, :].astype(F32)
+        hidden = hidden_ref[at, :].astype(F32)
+        rh = lax.rsqrt(jnp.mean(hidden * hidden, axis=-1, keepdims=True) + EPSILON)
+        weighted = d_normed * gain_ref[...]
+        inner_sum = jnp.sum(weighted * hidden, axis=-1, keepdims=True) / features
+        d_hidden_ref[at, :] = (
+            dout_ref[at, :].astype(F32) + rh * weighted - hidden * (rh * rh * rh) * inner_sum
+        )
+        return total + jnp.sum(d_normed * hidden * rh, axis=0, keepdims=True)
+
+    gain = lax.fori_loop(
+        0, hidden_ref.shape[0] // group, token_rows, jnp.zeros((1, features), F32)
+    )
+    flat[0:1, :] = gain[:, :half]
+    flat[1:2, :] = gain[:, half:]
+    gather = LineGather(flat, flat_all, ls, lr, ll)
+    gather.start()
+    for hop in range(1, gather.nz):
+        gather.relay(hop)
+    gather.finish()
+    total = flat_all[0]
+    for i in range(1, flat_all.shape[0]):
+        total = total + flat_all[i]
+    flat_ref[...] = total
+    shared_own[...] = total[0:8, :]
+    shared = QuadGather(shared_own, shared_all, qs, qr, ql)
+    shared.start()
+    one.finish()
+    shared.relay()
+    two.finish()
+    columns.finish()
+    shared.finish()
+    shared_ref[...] = shared_all[0] + shared_all[1] + shared_all[2] + shared_all[3]
+    own_columns = bc_ref.shape[1] // 4
+    for t in range(4):
+        bc_ref[:, t * own_columns : (t + 1) * own_columns] = bc_all[t, :, :own_columns]
+    dt_ref[...] = small_sum[:, own_columns : own_columns + dt_ref.shape[1]]
+
+
+def last_exchange(small, one, two, dx, hidden, d_out, gain, mix, scale, heads):
+    n, rows, width = small.shape
+    side = one.shape[2]
+    tokens, features = hidden.shape
+    half = mix.shape[1]
+    far = pl.BlockSpec(memory_space=pl.ANY)
+    near = pl.BlockSpec(memory_space=pltpu.VMEM)
+    shape = jax.ShapeDtypeStruct
+    return pl.pallas_call(
+        last_kernel,
+        name="last_exchange",
+        in_specs=[far] * 4 + [near] * 5,
+        out_specs=[near] * 7,
+        out_shape=[
+            shape((tokens, features), F32),
+            shape((rows, 2 * STATE), F32),
+            shape((rows, heads), F32),
+            shape((rows, side), F32),
+            shape((rows, side), F32),
+            shape(mix.shape, F32),
+            shape((8, half), F32),
+        ],
+        scratch_shapes=line_scatter_scratch(n, rows, width)
+        + line_scatter_scratch(n, rows, side)
+        + line_scatter_scratch(n, rows, side)
+        + quad_scatter_scratch(tokens, features)
+        + [
+            pltpu.VMEM(mix.shape, F32),
+            pltpu.VMEM((n,) + mix.shape, F32),
+            pltpu.VMEM((8, half), F32),
+            pltpu.VMEM((4, 8, half), F32),
+            pltpu.VMEM((rows, width), F32),
+            pltpu.VMEM((4, rows, width), F32),
+        ]
+        + line_semaphores(n)
+        + quad_semaphores()
+        + quad_semaphores(),
+        compiler_params=pltpu.CompilerParams(collective_id=3, has_side_effects=True),
+    )(small, one, two, dx, hidden, d_out, gain, mix, scale)
 
 
 def local(
@@ -604,72 +974,55 @@
     g_scale = jnp.sum(dyn * gated * r, axis=0)
     gy = d_gated * act
     d_gate = low(d_gated * y * (sig * (1.0 + gate * (1.0 - sig))))
-    g_out = low(dot(dout_all, yn, ((0,), (0,))))
-    g_gate = low(dot(xn, d_gate, ((0,), (0,))))
-    early = lax.psum_scatter(
-        jnp.concatenate([g_gate, g_out], 1), "dp", scatter_dimension=0, tiled=True
-    ).astype(F32)
-    partial_out = low(dot(yn, w_o, ((1,), (1,))))
-    branch = lax.psum_scatter(partial_out, "tensor", scatter_dimension=0, tiled=True)
-    hidden_own = hidden_in[0].astype(F32)
-    block_out = low(hidden_own + branch.astype(F32))
-
-    d_inner, d_dt, d_bc, g_x, g_bc, g_head = mixer_backward(
-        inner, small, gy, states, *params, dbc_dtype=BF16
+    n = lax.axis_size("dp")
+    g_out = low(dot(dout_all, yn, ((0,), (0,)))).reshape(n, own_width, -1)
+    g_gate = low(dot(xn, d_gate, ((0,), (0,)))).reshape(n, own_width, -1)
+    partial_out = low(dot(yn, w_o, ((1,), (1,)))).reshape(parts, rows_local, width)
+    d_inner, d_dt, d_bc, mix, gate_sum, out_sum, branch = mixer_backward(
+        inner, small, gy, states, *params, g_gate, g_out, partial_out
     )
-    d_bc_low = lax.psum(d_bc, "tensor")
+    block_out = low(hidden_in[0].astype(F32) + branch)
     own_columns = 2 * STATE // parts
-    d_bc_own = lax.dynamic_slice_in_dim(d_bc_low, tensor_index * own_columns, own_columns, 1)
-    late = jnp.concatenate([d_inner, d_bc_own, d_dt], 1)
-    g_late = low(dot(xn, late, ((0,), (0,))))
-    late_sum = lax.psum_scatter(g_late, "dp", scatter_dimension=0, tiled=True).astype(F32)
+    spare = jnp.zeros((inner.shape[0], 128 - own_columns - heads), BF16)
+    late_small = jnp.concatenate([d_bc.T, d_dt, spare], 1)
+    half = inner_local // 2
+    g_one = low(dot(xn, d_inner[:, :half], ((0,), (0,)))).reshape(n, own_width, -1)
+    g_two = low(dot(xn, d_inner[:, half:], ((0,), (0,)))).reshape(n, own_width, -1)
+    g_small = low(dot(xn, late_small, ((0,), (0,)))).reshape(n, own_width, -1)
     w_small_own = jnp.concatenate(
         [
             lax.dynamic_slice_in_dim(first, inner_local + tensor_index * own_columns, own_columns, 1),
-            w_small[:, 2 * STATE :],
+            first[:, inner_local + 2 * STATE : inner_local + 2 * STATE + 128 - own_columns],
         ],
         1,
     )
     d_xn = dot(d_gate, w_gate, ((1,), (1,))) + dot(d_inner, w_inner, ((1,), (1,)))
-    d_xn = d_xn + dot(late[:, inner_local:], w_small_own, ((1,), (1,)))
-    d_normed = lax.psum_scatter(low(d_xn), "tensor", scatter_dimension=0, tiled=True).astype(F32)
-    rh_own = lax.rsqrt(jnp.mean(hidden_own * hidden_own, axis=-1, keepdims=True) + EPSILON)
-    weighted = d_normed * gain
-    g_gain = jnp.sum(d_normed * hidden_own * rh_own, axis=0)
-    inner_sum = jnp.sum(weighted * hidden_own, axis=-1, keepdims=True)
-    d_hidden = (
-        d_out[0].astype(F32) + rh_own * weighted - hidden_own * (rh_own * rh_own * rh_own) * inner_sum / width
+    d_xn = low(d_xn + dot(late_small, w_small_own, ((1,), (1,)))).reshape(parts, rows_local, width)
+    d_hidden, g_w_bc, g_w_dt, left, right, flat, shared = last_exchange(
+        g_small, g_one, g_two, d_xn, hidden_in[0], d_out[0], gain, mix, g_scale[None], heads
     )
-    flat = jnp.concatenate(
-        [g_gain, g_bc.reshape(-1), g_x.reshape(-1), g_scale, g_head.reshape(-1)]
+    own = lax.dynamic_slice_in_dim(
+        shared[:2].reshape(-1), lax.axis_index("dp") * own_width, own_width, 0
     )
-    flat = lax.psum(flat, "dp")
-    shared_size = width + 5 * 2 * STATE
-    shared = lax.psum(flat[:shared_size], "tensor")
-    own = lax.dynamic_slice_in_dim(shared, lax.axis_index("dp") * in_gain.shape[0], in_gain.shape[0], 0)
-    g_bc = shared[width:].reshape(5, 2 * STATE)
-    g_x = flat[shared_size : shared_size + 5 * inner_local].reshape(5, inner_local)
-    rest = flat[shared_size + 5 * inner_local :]
-    g_scale = rest[:inner_local]
-    g_head = rest[inner_local:].reshape(3, heads)
-    g_w_bc = lax.all_gather(late_sum[:, inner_local : inner_local + own_columns], "tensor", axis=1, tiled=True)
-    g_zx = jnp.stack([early[:, :inner_local], late_sum[:, :inner_local]], 1)
+    g_bc = shared[2:4].reshape(-1)[: 5 * 2 * STATE].reshape(5, 2 * STATE)
+    g_x = flat[8:13]
+    g_zx = jnp.stack([gate_sum, jnp.concatenate([left, right], 1)], 1)
     return (
         block_out[None],
         d_hidden[None],
         own,
         g_zx,
-        late_sum[:, inner_local + own_columns :],
+        g_w_dt,
         g_w_bc,
-        early[:, inner_local:],
+        out_sum,
         g_x[:4],
         g_x[4],
         g_bc[:4],
         g_bc[4],
-        g_head[0],
-        g_head[1],
-        g_head[2],
-        g_scale,
+        flat[4, :heads],
+        flat[5, :heads],
+        flat[6, :heads],
+        flat[7],
     )
 
 

time: 492 us -> 327 us (0.66)
  waiting for transfers between devices: 182 us -> 0 us
  Pallas kernels: 132 us -> 227 us
  blocking collectives: 61.1 us -> 6 us
  between operations: 14.3 us -> 1.05 us
  local copies, waits for them, and re-layouts: 31.9 us -> 21.8 us
  matrix products: 49.7 us -> 55.5 us
    unnamed x7 -> x0, waiting for transfers between devices: 115 us -> none
    pallas_call x0 -> x1, Pallas kernels: none -> 58.9 us  [last_exchange(): pl.pallas_call(last_kernel, name='last_exchange', in_specs=[far] * 4 + [n...]
    psum x2 -> x0, blocking collectives: 47.3 us -> none  [the longest x1 37.1 us: local(): flat = lax.psum(flat, 'dp')]
    psum x1 -> x0, waiting for transfers between devices: 35.2 us -> none  [local(): d_bc_low = lax.psum(d_bc, 'tensor')]
    pallas_call x1, Pallas kernels: 27.4 us -> 60.2 us  [mixer_backward(): pl.pallas_call(backward_kernel, name='mixer_backward', grid=(blocks,), in...]
    reduce_scatter x2 -> x0, waiting for transfers between devices: 31.1 us -> none  [the longest x1 31.1 us: local(): lax.psum_scatter(low(d_xn), 'tensor', scatter_dimension=0, tiled=True)]
    unnamed x63 -> x76, local copies, waits for them, and re-layouts: 17.4 us -> 7.32 us
    mul x2 -> x0, other arithmetic: 7.25 us -> none  [the longest x1 7.24 us: local(): gy = d_gated * act]
  transfers between devices with their start and end apart: 5 -> 0, of which waited for: 4 -> 0; matrix products, arithmetic and copies ran while one was open for 10% -> 0% of each run, Pallas kernels for 0% -> 0%
where the time goes in v3:
time: 327 us
  Pallas kernels  227 us (69%)
  matrix products  55.5 us (17%)
  local copies, waits for them, and re-layouts  21.8 us (7%)
  other arithmetic  15.6 us (5%)
  blocking collectives  6 us (2%)
    pallas_call x1, Pallas kernels, mixer_backward(): pl.pallas_call(backward_kernel, name='mixer_backward', grid=(blocks,), in...  60.2 us
    pallas_call x1, Pallas kernels, last_exchange(): pl.pallas_call(last_kernel, name='last_exchange', in_specs=[far] * 4 + [n...  58.9 us
    pallas_call x1, Pallas kernels, mixer_forward(): pl.pallas_call(forward_kernel, name='mixer_forward', grid=(blocks,), in_s...  57.7 us
    dot_general x13, matrix products, dot(): lax.dot_general(a, b, (dims, ((), ())), precision=precision, preferred_el...  55.5 us
    pallas_call x1, Pallas kernels, gather_first(): pl.pallas_call(first_kernel, name='gather_first', in_specs=[whole, whole]...  50.2 us
    convert_element_type x2, other arithmetic, low(): return v.astype(BF16)  7.81 us
    unnamed x76, local copies, waits for them, and re-layouts  7.32 us

profile of v3, /device:TPU:0, one launch (start us, length us, event | category | flops | bytes accessed | tf_op | source)
XLA Modules:
  0.0 326.9 jit_solution(3508304259365856316)
XLA Ops:
  0.7 2.4 fusion.31
  5.0 50.2 %gather_first.1 = (bf16[8,192,1152]{2,1,0:T(8,128)(2,1)}, bf16[4,256,1536]{2,1,0:T(8,128)(2,1)}) custom-call(bf16[192,1152]{1,0:T(8,128)(2,1)} %concatenate.15.pack_ref, bf16[256,1536]{1,0:T(8,128)(2,1)} %bitcast.62), custom_call_target="tpu_custom_call" | custom-call | tf_op jit(solution)/shard_map/gather_first/pallas_call | solution.py:611
  56.8 2.6 multiply_reduce_fusion
  61.4 4.2 %fusion.12.inner_ref.prev_ref = f32[1024,768]{1,0:T(8,128)} fusion(bf16[1024,1536]{1,0:T(8,128)(2,1)S(1)} %fusion.1, bf16[1536,1152]{1,0:T(8,128)(2,1)S(1)} %bitcast.75), kind=kOutput, calls=%fused_computation.28 | convolution fusion | flops 2415919104 | bytes 8650752 | tf_op jit(solution)/shard_map/dot_general | solution.py:20
  65.7 2.9 fusion.15.small_ref.sprev_ref
  70.0 57.7 %mixer_forward.1 = (f32[1024,768]{1,0:T(8,128)}, f32[8,128,768]{2,1,0:T(8,128)}, bf16[8,192,1536]{2,1,0:T(8,128)(2,1)}, bf16[4,256,1536]{2,1,0:T(8,128)(2,1)}) custom-call(f32[1024,768]{1,0:T(8,128)} %fusion.12.inner_ref.prev_ref, f32[1024,268]{1,0:T(8,128)} %fusion.15.small_ref.sprev_ref, f32[4,768]{1,0:T(4,128)} %xw_ref.3, ...), custom_call_target="tpu_custom_call" | custom-call | flops 805306368 | bytes 12582912 | tf_op jit(solution)/shard_map/mixer_forward/pallas_call | solution.py:140
  127.8 4.4 %fusion.8 = f32[1024,768]{1,0:T(8,128)S(1)} fusion(bf16[1024,1536]{1,0:T(8,128)(2,1)S(1)} %copy-done.3, bf16[1536,1536]{1,0:T(8,128)(2,1)} %bitcast.97), kind=kOutput, calls=%fused_computation.24 | convolution fusion | flops 2415919104 | bytes 8650752 | tf_op jit(solution)/shard_map/dot_general | solution.py:20
  132.7 4.9 %multiply_reduce_fusion.3 = (f32[1024]{0:T(1024)S(1)}, f32[1024]{0:T(1024)S(1)}, f32[1024,768]{1,0:T(8,128)}, f32[1024,768]{1,0:T(8,128)}) fusion(f32[768]{0:T(1024)S(1)} %copy-done.24, f32[1024,768]{1,0:T(8,128)S(1)} %copy-done.5, f32[1024,768]{1,0:T(8,128)S(1)} %fusion.8, bf16[1024,1536]{1,0:T(8,128)(2,1)S(1)} %bitcast.105, ...), kind=kOutput, calls=%fused_computation.13 | convolution fusion | flops 2423781376 | bytes 18100224 | tf_op jit(solution)/shard_map/dot_general | solution.py:20
  137.6 6.0 %psum.7 = f32[2,1024]{1,0:T(2,128)S(1)} all-reduce(f32[2,1024]{1,0:T(2,128)S(1)} %pad_maximum_fusion.2), channel_id=1, replica_groups=mesh['dp'=8,'tensor'=4] {'tensor'}, use_global_device_ids=true, to_apply=%region_3.0 | all-reduce | flops 2048 | bytes 16384 | tf_op jit(solution)/shard_map/psum | solution.py:969
  143.6 7.0 %multiply_convert_fusion.1 = (bf16[1024,768]{1,0:T(8,128)(2,1)S(1)}, f32[1024,768]{1,0:T(8,128)}, f32[768]{0:T(1024)S(1)}) fusion(f32[1024,768]{1,0:T(8,128)} %copy-done.7, f32[1024,768]{1,0:T(8,128)} %get-tuple-element.37, f32[1024]{0:T(1024)S(1)} %bitcast.86, f32[1024,768]{1,0:T(8,128)} %get-tuple-element.89, f32[1024,768]{1,0:T(8,128)} %get-tuple-element.104, ...), kind=kLoop, calls=%fused_computation.10 | loop fusion | flops 16514304 | bytes 17319936 | tf_op jit(solution)/shard_map/convert_element_type | solution.py:24
  150.7 4.0 %convolution_convert_fusion.2 = bf16[1536,768]{1,0:T(8,128)(2,1)} fusion(bf16[1024,1536]{1,0:T(8,128)(2,1)S(1)} %copy-done.3, bf16[1024,768]{1,0:T(8,128)(2,1)S(1)} %get-tuple-element.90), kind=kOutput, calls=%fused_computation.7 | convolution fusion | flops 2417098752 | bytes 7077888 | tf_op jit(solution)/shard_map/dot_general | solution.py:20
  154.7 4.4 %convolution_convert_fusion.1 = bf16[1536,768]{1,0:T(8,128)(2,1)} fusion(bf16[1024,1536]{1,0:T(8,128)(2,1)S(1)} %bitcast.106, f32[1024,768]{1,0:T(8,128)S(1)} %copy-done.6, f32[1024]{0:T(1024)S(1)} %bitcast.83, f32[768]{0:T(1024)S(1)} %copy-done.24), kind=kOutput, calls=%fused_computation.6 | convolution fusion | flops 2419458048 | bytes 8657920 | tf_op jit(solution)/shard_map/dot_general | solution.py:20
  159.1 4.2 %convolution_convert_fusion = bf16[1024,1536]{1,0:T(8,128)(2,1)} fusion(bf16[1536,1536]{1,0:T(8,128)(2,1)S(1)} %bitcast.101, f32[1024,768]{1,0:T(8,128)S(1)} %copy-done.6, f32[1024]{0:T(1024)S(1)} %bitcast.84, f32[768]{0:T(1024)S(1)} %copy-done.24), kind=kOutput, calls=%fused_computation.5 | convolution fusion | flops 2419851264 | bytes 8658944 | tf_op jit(solution)/shard_map/dot_general | solution.py:20
  163.3 60.2 %mixer_backward.1 = (bf16[1024,768]{1,0:T(8,128)(2,1)}, bf16[1024,12]{1,0:T(8,128)(2,1)}, bf16[64,1024]{1,0:T(8,128)(2,1)}, f32[16,768]{1,0:T(8,128)}, f32[192,7...) custom-call(f32[1024,768]{1,0:T(8,128)} %fusion.12.inner_ref.prev_ref, f32[1024,768]{1,0:T(8,128)} %fusion.12.inner_ref.prev_ref, ...), custom_call_target="tpu_custom_call" | custom-call | flops 2013265920 | bytes 15728640 | tf_op jit(solution)/shard_map/mixer_backward/pallas_call | solution.py:380
  223.5 2.5 fusion.17
  226.9 3.9 %convolution_convert_fusion.5 = bf16[1536,128]{1,0:T(8,128)(2,1)} fusion(bf16[1024,1536]{1,0:T(8,128)(2,1)} %copy-done.2, bf16[1024,12]{0,1:T(8,128)(2,1)} %copy.53, bf16[1024,64]{0,1:T(8,128)(2,1)S(1)} %bitcast.80, bf16[128]{0:T(256)(128)(2,1)S(1)} %pad.8.clone), kind=kOutput, calls=%fused_computation.18 | convolution fusion | flops 403636224 | bytes 3694848 | tf_op jit(solution)/shard_map/dot_general | solution.py:20
  230.9 2.8 convolution_convert_fusion.4
  233.7 2.8 convolution_convert_fusion.3
  236.6 4.7 %fusion.6 = f32[1024,1536]{1,0:T(8,128)} fusion(bf16[1024,768]{1,0:T(8,128)(2,1)S(1)} %copy-done.10, bf16[1536,1536]{1,0:T(8,128)(2,1)S(1)} %bitcast.104), kind=kOutput, calls=%fused_computation.22 | convolution fusion | flops 2415919104 | bytes 10223616 | tf_op jit(solution)/shard_map/dot_general | solution.py:20
  241.3 4.5 %fusion.10 = f32[1024,1536]{1,0:T(8,128)} fusion(bf16[1024,768]{1,0:T(8,128)(2,1)S(1)} %copy-done.26, bf16[1536,1152]{1,0:T(8,128)(2,1)S(1)} %bitcast.77), kind=kOutput, calls=%fused_computation.26 | convolution fusion | flops 2415919104 | bytes 10223616 | tf_op jit(solution)/shard_map/dot_general | solution.py:20
  246.0 7.5 %add_convert_fusion = bf16[1024,1536]{1,0:T(8,128)(2,1)} fusion(f32[1024,1536]{1,0:T(8,128)} %fusion.6, f32[1024,1536]{1,0:T(8,128)} %fusion.10, bf16[1536,64]{1,0:T(8,128)(2,1)S(1)} %get-tuple-element.94, bf16[1536,64]{1,0:T(8,128)(2,1)S(1)} %get-tuple-element.93, bf16[1024,12]{0,1:T(8,128)(2,1)} %copy.53, bf16[1024,64]{0,1:T(8,128)(2,1)} %bitcast.79, ...), kind=kOutput, calls=%fused_computation.3 | convolution fusion | flops 408944640 | bytes 16277760 | tf_op jit(solution)/shard_map/dot_general | solution.py:20
  254.8 58.9 %last_exchange.1 = (f32[256,1536]{1,0:T(8,128)}, f32[192,256]{1,0:T(8,128)}, f32[192,12]{1,0:T(8,128)}, f32[192,384]{1,0:T(8,128)}, f32[192,384]{1,0:T(8,128)}, /*index=5*/f32[16,768]{1,0:T(8,128)}, f32[8,768]{1,0:T(8,128)}) custom-call(bf16[8,192,128]{2,1,0:T(8,128)(2,1)} %bitcast.73, bf16[8,192,384]{2,1,0:T(8,128)(2,1)} %bitcast.68, ...), custom_call_target="tpu_custom_call" | custom-call | tf_op jit(solution)/shard_map/last_exchange/pallas_call | solution.py:897
  316.4 1.9 copy.54
  320.4 1.4 slice_reduce_fusion
  (107 shorter events, 19.5 us)
Async XLA Ops:
  55.3 4.1 %copy-start = (bf16[4,256,1536]{2,1,0:T(8,128)(2,1)S(1)}, bf16[4,256,1536]{2,1,0:T(8,128)(2,1)}, u32[]{:S(2)}) copy-start(bf16[4,256,1536]{2,1,0:T(8,128)(2,1)} %get-tuple-element.35) | copy-start | bytes 9437188
  61.4 4.2 %copy-start.2 = (bf16[1024,1536]{1,0:T(8,128)(2,1)}, bf16[1024,1536]{1,0:T(8,128)(2,1)S(1)}, u32[]{:S(2)}) copy-start(bf16[1024,1536]{1,0:T(8,128)(2,1)S(1)} %fusion.1) | copy-start | bytes 9437188
  65.7 3.5 %copy-start.16 = (bf16[192,768]{1,0:T(8,128)(2,1)S(1)}, bf16[192,768]{1,0:T(8,128)(2,1)}, u32[]{:S(2)}) copy-start(bf16[192,768]{1,0:T(8,128)(2,1)} %param.21) | copy-start | bytes 884740
  70.0 57.7 %copy-start.3 = (bf16[1024,1536]{1,0:T(8,128)(2,1)S(1)}, bf16[1024,1536]{1,0:T(8,128)(2,1)}, u32[]{:S(2)}) copy-start(bf16[1024,1536]{1,0:T(8,128)(2,1)} %copy-done.2) | copy-start | bytes 9437188
  127.7 4.5 %copy-start.5 = (f32[1024,768]{1,0:T(8,128)S(1)}, f32[1024,768]{1,0:T(8,128)}, u32[]{:S(2)}) copy-start(f32[1024,768]{1,0:T(8,128)} %get-tuple-element.37) | copy-start | bytes 9437188
  127.7 4.5 %copy-start.24 = (f32[768]{0:T(1024)S(1)}, f32[768]{0:T(1024)}, u32[]{:S(2)}) copy-start(f32[768]{0:T(1024)} %param.29) | copy-start | bytes 9220
  127.7 4.5 %copy-start.27 = (bf16[8,192,1536]{2,1,0:T(8,128)(2,1)S(1)}, bf16[8,192,1536]{2,1,0:T(8,128)(2,1)}, u32[]{:S(2)}) copy-start(bf16[8,192,1536]{2,1,0:T(8,128)(2,1)} %get-tuple-element.38) | copy-start | bytes 14155780
  127.8 4.9 %copy-start.28 = (bf16[4,256,1536]{2,1,0:T(8,128)(2,1)S(1)}, bf16[4,256,1536]{2,1,0:T(8,128)(2,1)}, u32[]{:S(2)}) copy-start(bf16[4,256,1536]{2,1,0:T(8,128)(2,1)} %get-tuple-element.39) | copy-start | bytes 9437188
  132.2 5.4 %copy-start.7 = (f32[1024,768]{1,0:T(8,128)}, f32[1024,768]{1,0:T(8,128)S(1)}, u32[]{:S(2)}) copy-start(f32[1024,768]{1,0:T(8,128)S(1)} %fusion.8) | copy-start | bytes 9437188
  150.7 4.0 %copy-start.9 = (bf16[1024,768]{1,0:T(8,128)(2,1)}, bf16[1024,768]{1,0:T(8,128)(2,1)S(1)}, u32[]{:S(2)}) copy-start(bf16[1024,768]{1,0:T(8,128)(2,1)S(1)} %get-tuple-element.90) | copy-start | bytes 4718596
  150.7 4.0 %copy-start.6 = (f32[1024,768]{1,0:T(8,128)S(1)}, f32[1024,768]{1,0:T(8,128)}, u32[]{:S(2)}) copy-start(f32[1024,768]{1,0:T(8,128)} %get-tuple-element.89) | copy-start | bytes 9437188
  150.7 4.0 %copy-start.29 = (bf16[4,256,1536]{2,1,0:T(8,128)(2,1)S(1)}, bf16[4,256,1536]{2,1,0:T(8,128)(2,1)}, u32[]{:S(2)}) copy-start(bf16[4,256,1536]{2,1,0:T(8,128)(2,1)} %get-tuple-element.39) | copy-start | bytes 9437188
  150.7 8.4 %slice-start = ((s8[4718592]{0:T(1024)(128)(4,1)}), s8[4194304]{0:T(1024)(128)(4,1)S(1)}, s32[]{:S(2)}) async-start(s8[4718592]{0:T(1024)(128)(4,1)} %bitcast.99), calls=%async_computation | async-start | bytes 8388608
  154.7 4.5 %slice-start.1 = ((s8[4718592]{0:T(1024)(128)(4,1)}), s8[524288]{0:T(1024)(128)(4,1)S(1)}, s32[]{:S(2)}) async-start(s8[4718592]{0:T(1024)(128)(4,1)} %bitcast.99), calls=%async_computation.1 | async-start | bytes 1048576
  163.3 60.2 %copy-start.1 = (bf16[1,256,1536]{2,1,0:T(8,128)(2,1)S(1)}, bf16[1,256,1536]{2,1,0:T(8,128)(2,1)}, u32[]{:S(2)}) copy-start(bf16[1,256,1536]{2,1,0:T(8,128)(2,1)} %param.15) | copy-start | bytes 2359300
  226.1 4.8 %copy-start.4 = (bf16[1024,1536]{1,0:T(8,128)(2,1)S(1)}, bf16[1024,1536]{1,0:T(8,128)(2,1)}, u32[]{:S(2)}) copy-start(bf16[1024,1536]{1,0:T(8,128)(2,1)} %copy-done.2) | copy-start | bytes 9437188
  226.8 4.0 %copy-start.26 = (bf16[1024,768]{1,0:T(8,128)(2,1)S(1)}, bf16[1024,768]{1,0:T(8,128)(2,1)}, u32[]{:S(2)}) copy-start(bf16[1024,768]{1,0:T(8,128)(2,1)} %get-tuple-element.44) | copy-start | bytes 4718596
  230.9 5.7 %slice-start.2 = ((s8[4718592]{0:T(1024)(128)(4,1)}), s8[4194304]{0:T(1024)(128)(4,1)S(1)}, s32[]{:S(2)}) async-start(s8[4718592]{0:T(1024)(128)(4,1)} %bitcast.102), calls=%async_computation.2 | async-start | bytes 8388608
  236.6 4.7 %copy-start.15 = (bf16[8,192,1152]{2,1,0:T(8,128)(2,1)S(1)}, bf16[8,192,1152]{2,1,0:T(8,128)(2,1)}, u32[]{:S(2)}) copy-start(bf16[8,192,1152]{2,1,0:T(8,128)(2,1)} %get-tuple-element.36) | copy-start | bytes 10616836
  254.7 61.6 %copy-start.13 = (f32[192,768]{1,0:T(8,128)S(1)}, f32[192,768]{1,0:T(8,128)}, u32[]{:S(2)}) copy-start(f32[192,768]{1,0:T(8,128)} %get-tuple-element.48) | copy-start | bytes 1769476
  313.6 4.7 %copy-start.20 = (f32[192,12]{1,0:T(8,128)S(1)}, f32[192,12]{1,0:T(8,128)}, u32[]{:S(2)}) copy-start(f32[192,12]{1,0:T(8,128)} %get-tuple-element.74) | copy-start | bytes 27652
  313.7 10.6 %copy-start.8 = (f32[256,1536]{1,0:T(8,128)S(1)}, f32[256,1536]{1,0:T(8,128)}, u32[]{:S(2)}) copy-start(f32[256,1536]{1,0:T(8,128)} %get-tuple-element.46) | copy-start | bytes 4718596
  316.4 9.0 %copy-start.18 = (f32[192,256]{1,0:T(8,128)S(1)}, f32[192,256]{1,0:T(8,128)}, u32[]{:S(2)}) copy-start(f32[192,256]{1,0:T(8,128)} %get-tuple-element.127) | copy-start | bytes 589828
  316.4 9.7 %copy-start.12 = (f32[192,768]{1,0:T(8,128)S(1)}, f32[192,768]{1,0:T(8,128)}, u32[]{:S(2)}) copy-start(f32[192,768]{1,0:T(8,128)} %get-tuple-element.128) | copy-start | bytes 1769476
  (10 other events, 30.2 us)
